TPU v7x, 32 devices: a whole 2x2x4 slice. The times are simulated.
32 devices in a mesh: clip: 2 (over y), tm: 4 (over z), space: 2 (over x), chan: 2 (over core).
Axes of the slice: x: 2, y: 2, z: 4, core: 2. Of those that a mesh axis runs over, the one named last changes fastest.
Arguments:
- features: bfloat16 [16, 8, 90, 256], P(('clip', 'tm'), 'space'), parts along dimension 0, may hold values from -700 to 700
- hidden: bfloat16 [16, 8, 90, 256], P(('clip', 'tm'), 'space'), parts along dimension 0, may hold values from -700 to 700
- cotangent: bfloat16 [16, 8, 90, 256], P(('clip', 'tm'), 'space'), parts along dimension 0, may hold values from -6 to 6
- kernel_one: bfloat16 [256, 3, 3, 3, 256], P(None, None, None, None, 'chan'), may hold values from -0.078125 to 0.078125
- kernel_two: bfloat16 [256, 3, 3, 3, 256], P(None, None, None, None, 'chan'), may hold values from -0.078125 to 0.078125
- gains: float32 [2, 256], replicated, may hold values from 0.25 to 1.75
Outputs:
- feature_grad: bfloat16 [16, 8, 90, 256], P(('clip', 'tm'), 'space', None, 'chan'), parts along dimension 0
- delta_one: float32 [512, 3, 3, 3, 256], P(('clip', 'tm', 'space'), None, None, None, 'chan'), parts along dimension 0
- delta_two: float32 [512, 3, 3, 3, 256], P(('clip', 'tm', 'space'), None, None, None, 'chan'), parts along dimension 0
- gain_grads: float32 [4, 256], P('clip', 'chan'), parts along dimension 0
There are 2 independent parts, one for each index of `clip`. A program takes and returns all parts, laid end to end along the dimension named above; an argument that names none is the same for every part. Nothing has to cross between parts.
All inputs are finite; a program needn't handle non-finite values.
Results may differ from a plain program's by a relative error of at most 0.005.
Values may be sent and summed in bfloat16 or wider, within the bound.
A program may use at most 128 MiB of HBM per device.

v0:
```python
import functools

import jax
import jax.numpy as jnp
from jax import lax
from jax.experimental import pallas as pl
from jax.experimental.pallas import tpu as pltpu
from jax.sharding import PartitionSpec as P

GROUPS = 32
EPS = 1e-06
MESH = pl.DeviceIdType.MESH
F32 = jnp.float32
BF16 = jnp.bfloat16


def group_sums(values, per):
    channels = values.shape[1]
    row = lax.broadcasted_iota(jnp.int32, (channels, channels), 0) // per
    col = lax.broadcasted_iota(jnp.int32, (channels, channels), 1) // per
    same = jnp.where(row == col, 1.0, 0.0).astype(F32)
    return jnp.dot(values, same, precision=lax.Precision.HIGHEST, preferred_element_type=F32)


def body(
    sizes,
    f_ref, h_ref, cot_ref, k1_ref, k2_ref, gain_ref,
    fg_ref, d1_ref, d2_ref, w_ref,
    ext2, ext1, gh, taps, act1, act2, acc,
    xs2, xr2, xs1, xr1, vec, r0, r2, r1, dd2, dd1, rr2, rr1,
    halo_s, halo_r, xsem_s, xsem_r, ar_s, ar_r, dl_s, dl_r,
):
    width, n_t, n_s = sizes
    frames, height, padded, half = cot_ref.shape
    channels = f_ref.shape[3]
    per = channels // GROUPS
    n = n_t * n_s
    rows = frames * height * padded
    block = height * padded
    share = channels // n
    t = lax.axis_index("tm")
    s = lax.axis_index("space")
    chan = lax.axis_index("chan")
    partner = 1 - chan
    rank = t * n_s + s
    members = float(frames * height * width * per * n)
    mine = pl.ds(pl.multiple_of(chan * half, half), half)
    theirs = pl.ds(pl.multiple_of(partner * half, half), half)

    def place(j):
        return {"tm": j // n_s, "space": lax.rem(j, n_s)}

    def peer(k):
        return lax.rem(rank + k, n)

    def each_peer(fn):
        def step(k, carry):
            fn(k)
            return carry

        lax.fori_loop(1, n, step, 0)

    ext2[...] = jnp.zeros_like(ext2)
    ext1[...] = jnp.zeros_like(ext1)

    barrier = pltpu.get_barrier_semaphore()
    pl.semaphore_signal(barrier, inc=1, device_id={"chan": partner}, device_id_type=MESH)
    each_peer(
        lambda k: pl.semaphore_signal(barrier, inc=1, device_id=place(peer(k)), device_id_type=MESH)
    )
    pl.semaphore_wait(barrier, n)

    last = height - 1
    below = (slice(0, frames), slice(height + 1, height + 2))
    above = (slice(0, frames), slice(0, 1))
    later = slice(frames, frames + 2)
    moves = (
        (0, -1, (slice(0, frames), slice(0, 1)), below),
        (0, 1, (slice(0, frames), slice(last, last + 1)), above),
        (-1, 0, (slice(0, 2), slice(0, height)), (later, slice(1, height + 1))),
        (-1, -1, (slice(0, 2), slice(0, 1)), (later, slice(height + 1, height + 2))),
        (-1, 1, (slice(0, 2), slice(last, last + 1)), (later, slice(0, 1))),
    )

    def inside(dt, ds):
        ok = None
        for value, step, count in ((t, dt, n_t), (s, ds, n_s)):
            if step:
                now = (value + step >= 0) & (value + step < count)
                ok = now if ok is None else ok & now
        return ok

    def halo(layer, source, dest, m):
        dt, ds, src, dst = moves[m]
        return pltpu.make_async_remote_copy(
            src_ref=source.at[src], dst_ref=dest.at[dst],
            send_sem=halo_s.at[layer, m], recv_sem=halo_r.at[layer, m],
            device_id={"tm": t + dt, "space": s + ds}, device_id_type=MESH,
        )

    def halo_start(layer, source, dest):
        for m in (2, 0, 1, 3, 4):
            @pl.when(inside(moves[m][0], moves[m][1]))
            def _(m=m):
                halo(layer, source, dest, m).start()

    def halo_arrive(layer, source, dest):
        for m in (2, 0, 1, 3, 4):
            @pl.when(inside(-moves[m][0], -moves[m][1]))
            def _(m=m):
                halo(layer, source, dest, m).wait_recv()

    def halo_end(layer, source, dest):
        for m in (2, 0, 1, 3, 4):
            @pl.when(inside(moves[m][0], moves[m][1]))
            def _(m=m):
                halo(layer, source, dest, m).wait_send()

    def sums_copy(layer, buf, k, slot):
        return pltpu.make_async_remote_copy(
            src_ref=buf.at[slot], dst_ref=buf.at[slot],
            send_sem=ar_s.at[layer, k], recv_sem=ar_r.at[layer, slot],
            device_id=place(peer(k)), device_id_type=MESH,
        )

    def sums_start(layer, buf, values):
        buf[rank] = values
        each_peer(lambda k: sums_copy(layer, buf, k, rank).start())

    def sums_finish(layer, buf):
        each_peer(lambda k: sums_copy(layer, buf, k, peer(k)).wait_recv())
        return jnp.sum(buf[...], axis=0)

    def sums_end(layer, buf):
        each_peer(lambda k: sums_copy(layer, buf, k, rank).wait_send())

    def share_copy(layer, out, buf, k, target, slot):
        return pltpu.make_async_remote_copy(
            src_ref=out.at[target], dst_ref=buf.at[slot],
            send_sem=dl_s.at[layer, k], recv_sem=dl_r.at[layer, slot],
            device_id=place(peer(k)), device_id_type=MESH,
        )

    def cross(layer, source, dest, f):
        return pltpu.make_async_remote_copy(
            src_ref=source.at[f], dst_ref=dest.at[f],
            send_sem=xsem_s.at[layer, f], recv_sem=xsem_r.at[layer, f],
            device_id={"chan": partner}, device_id_type=MESH,
        )

    column = lax.rem(lax.broadcasted_iota(jnp.int32, (rows, 1), 0), padded)
    real = column < width

    halo_start(0, cot_ref, ext2)
    ext2[0:frames, 1 : height + 1] = cot_ref[...]
    field_one = f_ref[...].reshape(rows, channels).astype(F32)
    field_two = h_ref[...].reshape(rows, channels).astype(F32)
    parts = [
        jnp.sum(field_one, axis=0, keepdims=True),
        jnp.sum(field_one * field_one, axis=0, keepdims=True),
        jnp.sum(field_two, axis=0, keepdims=True),
        jnp.sum(field_two * field_two, axis=0, keepdims=True),
        jnp.zeros((4, channels), F32),
    ]
    sums_start(0, r0, jnp.concatenate(parts, axis=0))

    def fill_taps(ext):
        def step(f, carry):
            cells = ext[f].reshape((height + 2) * padded, half).astype(F32)
            size = cells.shape[0]
            ahead = pltpu.roll(cells, size - 1, 0)
            behind = pltpu.roll(cells, 1, 0)
            for c, value in enumerate((ahead, cells, behind)):
                taps[f, :, :, c * half : (c + 1) * half] = value.astype(BF16).reshape(
                    height + 2, padded, half
                )
            return carry

        lax.fori_loop(0, frames + 2, step, 0)

    def conv(kernel, layer, source, dest):
        def step(f, carry):
            total = None
            for ab in range(9):
                a, b = ab // 3, ab % 3
                left = taps[2 - a + f, 2 - b : 2 - b + height].reshape(block, 3 * half)
                term = lax.dot_general(
                    left, kernel[ab], (((1,), (1,)), ((), ())), preferred_element_type=F32
                )
                total = term if total is None else total + term
            acc[f] = total
            source[f] = acc[f, :, theirs].astype(BF16)
            cross(layer, source, dest, f).start()
            return carry

        lax.fori_loop(0, frames, step, 0)

    def delta(act, out, own):
        def step(ab, carry):
            a = ab // 3
            b = lax.rem(ab, 3)
            right = taps[pl.ds(2 - a, frames), pl.ds(2 - b, height)].reshape(rows, 3 * half)
            product = jnp.dot(act[...], right, preferred_element_type=F32)
            small = product.astype(BF16)
            for j in range(n):
                out[j, ab] = small[j * share : (j + 1) * share]

                @pl.when(rank == j)
                def _(j=j):
                    own[ab] = product[j * share : (j + 1) * share]

            return carry

        lax.fori_loop(0, 9, step, 0)

    halo_arrive(0, cot_ref, ext2)
    fill_taps(ext2)
    conv(k2_ref, 0, xs2, xr2)

    totals = group_sums(sums_finish(0, r0), per) / members
    mean_one, mean_two = totals[0:1], totals[2:3]
    scale_one = lax.rsqrt(totals[1:2] - mean_one * mean_one + EPS)
    scale_two = lax.rsqrt(totals[3:4] - mean_two * mean_two + EPS)
    vec[0:1] = mean_one
    vec[1:2] = scale_one
    vec[2:3] = gain_ref[0:1]
    vec[3:4] = mean_two
    vec[4:5] = scale_two
    vec[5:6] = gain_ref[1:2]

    def activate(field_ref, base, act):
        field = field_ref[...].reshape(rows, channels).astype(F32)
        scaled = (field - vec[base : base + 1]) * vec[base + 1 : base + 2] * vec[base + 2 : base + 3]
        active = jnp.where(real, scaled * jax.nn.sigmoid(scaled), 0.0)
        act[...] = active.T.astype(BF16)

    activate(h_ref, 3, act2)
    delta(act2, dd2, d2_ref)

    def norm_back(field_ref, base, layer, dest, buf, w_row):
        for f in range(frames):
            cross(layer, xs2 if layer == 0 else xs1, dest, f).wait_recv()
        upstream = acc[:, :, mine].reshape(rows, half) + dest[...].reshape(rows, half).astype(F32)
        field = field_ref[:, :, :, mine].reshape(rows, half).astype(F32)
        scale = vec[base + 1 : base + 2, mine]
        gain = vec[base + 2 : base + 3, mine]
        centred = (field - vec[base : base + 1, mine]) * scale
        scaled = centred * gain
        gate = jax.nn.sigmoid(scaled)
        slope = jnp.where(real, upstream * gate * (1.0 + scaled * (1.0 - gate)), 0.0)
        parts = [
            jnp.sum(slope, axis=0, keepdims=True),
            jnp.sum(slope * centred, axis=0, keepdims=True),
            jnp.zeros((6, half), F32),
        ]
        sums_start(layer + 1, buf, jnp.concatenate(parts, axis=0))
        totals = sums_finish(layer + 1, buf)
        w_ref[w_row : w_row + 1] = totals[1:2]
        means = group_sums(totals * gain, per) / members
        grad = scale * (slope * gain - means[0:1] - centred * means[1:2])
        return jnp.where(real, grad, 0.0)

    grad_hidden = norm_back(h_ref, 3, 0, xr2, r2, 1).astype(BF16)
    gh[...] = grad_hidden.reshape(frames, height, padded, half)
    halo_start(1, gh, ext1)
    each_peer(lambda k: share_copy(0, dd2, rr2, k, peer(k), rank).start())
    ext1[0:frames, 1 : height + 1] = gh[...]
    activate(f_ref, 0, act1)
    halo_arrive(1, gh, ext1)
    fill_taps(ext1)
    conv(k1_ref, 1, xs1, xr1)
    delta(act1, dd1, d1_ref)
    each_peer(lambda k: share_copy(1, dd1, rr1, k, peer(k), rank).start())
    grad = norm_back(f_ref, 0, 1, xr1, r1, 0)
    fg_ref[...] = (cot_ref[...].reshape(rows, half).astype(F32) + grad).astype(BF16)

    def collect(layer, out, buf, own):
        def step(k, carry):
            share_copy(layer, out, buf, k, peer(k), peer(k)).wait_recv()
            own[...] += buf[peer(k)].astype(F32)
            return carry

        lax.fori_loop(1, n, step, 0)

    collect(0, dd2, rr2, d2_ref)
    collect(1, dd1, rr1, d1_ref)

    halo_end(0, cot_ref, ext2)
    halo_end(1, gh, ext1)
    sums_end(0, r0)
    sums_end(1, r2)
    sums_end(2, r1)
    for f in range(frames):
        cross(0, xs2, xr2, f).wait_send()
        cross(1, xs1, xr1, f).wait_send()
    each_peer(lambda k: share_copy(0, dd2, rr2, k, peer(k), rank).wait_send())
    each_peer(lambda k: share_copy(1, dd1, rr1, k, peer(k), rank).wait_send())


def shards(n_t, n_s, features, hidden, cotangent, kernel_one, kernel_two, gains):
    frames, height, width, channels = features.shape
    half = kernel_one.shape[4]
    padded = -(-width // 16) * 16
    if padded < width + 1:
        padded += 16
    n = n_t * n_s
    share = channels // n
    rows = frames * height * padded
    block = height * padded
    offset = lax.axis_index("chan") * half

    def wide(field):
        return jnp.pad(field, ((0, 0), (0, 0), (0, padded - width), (0, 0)))

    def stacked(kernel):
        return kernel.reshape(channels, 9, 3 * half).transpose(1, 0, 2)

    cot = wide(lax.dynamic_slice_in_dim(cotangent, offset, half, 3))
    vmem = pl.BlockSpec(memory_space=pltpu.VMEM)
    ext = pltpu.VMEM((frames + 2, height + 2, padded, half), BF16)
    halves = pltpu.VMEM((frames, block, half), BF16)
    pieces = pltpu.VMEM((n, 9, share, 3 * half), BF16)
    dma = pltpu.SemaphoreType.DMA
    grad, delta_one, delta_two, weighted = pl.pallas_call(
        functools.partial(body, (width, n_t, n_s)),
        out_shape=(
            jax.ShapeDtypeStruct((rows, half), BF16),
            jax.ShapeDtypeStruct((9, share, 3 * half), F32),
            jax.ShapeDtypeStruct((9, share, 3 * half), F32),
            jax.ShapeDtypeStruct((2, half), F32),
        ),
        in_specs=[vmem] * 6,
        out_specs=(vmem,) * 4,
        scratch_shapes=[
            ext,
            ext,
            pltpu.VMEM((frames, height, padded, half), BF16),
            pltpu.VMEM((frames + 2, height + 2, padded, 3 * half), BF16),
            pltpu.VMEM((channels, rows), BF16),
            pltpu.VMEM((channels, rows), BF16),
            pltpu.VMEM((frames, block, channels), F32),
            halves,
            halves,
            halves,
            halves,
            pltpu.VMEM((8, channels), F32),
            pltpu.VMEM((n, 8, channels), F32),
            pltpu.VMEM((n, 8, half), F32),
            pltpu.VMEM((n, 8, half), F32),
            pieces,
            pieces,
            pieces,
            pieces,
            dma((2, 5)),
            dma((2, 5)),
            dma((2, frames)),
            dma((2, frames)),
            dma((3, n)),
            dma((3, n)),
            dma((2, n)),
            dma((2, n)),
        ],
        compiler_params=pltpu.CompilerParams(
            collective_id=0, has_side_effects=True, vmem_limit_bytes=63 * 1024 * 1024
        ),
    )(wide(features), wide(hidden), cot, stacked(kernel_one), stacked(kernel_two), gains)

    def unstacked(delta):
        return delta.transpose(1, 0, 2).reshape(share, 3, 3, 3, half)

    feature_grad = grad.reshape(frames, height, padded, half)[:, :, :width]
    return (feature_grad, unstacked(delta_one), unstacked(delta_two), weighted)


def solution(mesh):
    placed = (
        P(("clip", "tm"), "space", None, None),
        P(("clip", "tm"), "space", None, None),
        P(("clip", "tm"), "space", None, None),
        P(None, None, None, None, "chan"),
        P(None, None, None, None, "chan"),
        P(),
    )
    return jax.shard_map(
        functools.partial(shards, mesh.shape["tm"], mesh.shape["space"]),
        mesh=mesh,
        in_specs=placed,
        out_specs=(
            P(("clip", "tm"), "space", None, "chan"),
            P(("clip", "tm", "space"), None, None, None, "chan"),
            P(("clip", "tm", "space"), None, None, None, "chan"),
            P("clip", "chan"),
        ),
        check_vma=False,
    )
```

profile of v0, /device:TPU:0, one launch (start us, length us, event | category | flops | bytes accessed | tf_op | source)
XLA Modules:
  0.0 130.0 jit_solution(15392125585109324736)
XLA Ops:
  0.6 0.0 copy-start
  0.6 1.0 copy-done
  1.6 0.1 constant_dynamic-slice_fusion
  1.7 0.7 pad.13.cot_ref
  2.4 2.6 %copy.21 = bf16[256,3,3,3,128]{0,4,3,2,1:T(8,128)(2,1)S(1)} copy(bf16[256,3,3,3,128]{4,0,3,2,1:T(8,128)(2,1)} %param.9) | data formatting | bytes 3538944 | tf_op args[3]
  5.1 2.3 %copy.22 = bf16[256,9,384]{2,0,1:T(8,128)(2,1)} copy(bf16[256,9,384]{0,2,1:T(8,128)(2,1)S(1)} %bitcast.12) | data formatting | bytes 3538944 | tf_op jit(solution)/shard_map/reshape | solution.py:316
  7.3 2.6 %copy.23 = bf16[256,3,3,3,128]{0,4,3,2,1:T(8,128)(2,1)S(1)} copy(bf16[256,3,3,3,128]{4,0,3,2,1:T(8,128)(2,1)} %param.10) | data formatting | bytes 3538944 | tf_op args[4]
  9.9 0.0 copy-start.2
  10.0 0.0 copy-start.3
  10.0 2.2 %copy.24 = bf16[256,9,384]{2,0,1:T(8,128)(2,1)} copy(bf16[256,9,384]{0,2,1:T(8,128)(2,1)S(1)} %bitcast.13) | data formatting | bytes 3538944 | tf_op jit(solution)/shard_map/reshape | solution.py:316
  12.2 0.0 copy-done.2
  12.2 0.8 pad.11.f_ref
  13.0 0.0 copy-done.3
  13.1 0.8 pad.12.h_ref
  13.9 111.7 %shard_map.93 = (bf16[768,128]{1,0:T(8,128)(2,1)}, f32[9,32,384]{2,1,0:T(8,128)}, f32[9,32,384]{2,1,0:T(8,128)}, f32[2,128]{1,0:T(2,128)}) custom-call(bf16[2,4,96,256]{3,2,1,0:T(8,128)(2,1)} %pad.11.f_ref, bf16[2,4,96,256]{3,2,1,0:T(8,128)(2,1)} %pad.12.h_ref, bf16[2,4,96,128]{3,2,1,0:T(8,128)(2,1)} %pad.13.cot_ref, bf16[9,256,384]{2,1,0:T(8,128)(2,1)} %bitcast.14, ...), custom_call_target="tpu_custom_call" | custom-call | tf_op jit(solution)/shard_map/pallas_call | solution.py:324
  125.6 0.0 copy-start.1
  125.6 1.2 reshape.26
  126.8 0.0 copy-start.4
  126.8 0.0 copy-start.5
  126.8 0.8 copy.26
  127.7 0.0 copy-done.1
  127.7 0.2 reshape.27
  127.8 0.8 copy.27
  128.6 0.0 copy-done.4
  128.7 0.8 copy.29
  129.4 0.0 copy-done.5
  129.4 0.6 copy.31
  (3 shorter events, 0.1 us)
Async XLA Ops:
  0.6 1.0 copy-start
  9.9 2.3 %copy-start.2 = (bf16[2,4,90,256]{3,1,2,0:T(4,128)(2,1)S(1)}, bf16[2,4,90,256]{3,1,2,0:T(4,128)(2,1)}, u32[]{:S(2)}) copy-start(bf16[2,4,90,256]{3,1,2,0:T(4,128)(2,1)} %param.6) | copy-start | bytes 1105924
  10.0 3.1 %copy-start.3 = (bf16[2,4,90,256]{3,1,2,0:T(4,128)(2,1)S(1)}, bf16[2,4,90,256]{3,1,2,0:T(4,128)(2,1)}, u32[]{:S(2)}) copy-start(bf16[2,4,90,256]{3,1,2,0:T(4,128)(2,1)} %param.7) | copy-start | bytes 1105924
  125.6 2.1 %copy-start.1 = (f32[9,32,384]{2,1,0:T(8,128)S(1)}, f32[9,32,384]{2,1,0:T(8,128)}, u32[]{:S(2)}) copy-start(f32[9,32,384]{2,1,0:T(8,128)} %get-tuple-element.10) | copy-start | bytes 1327108
  126.8 1.8 %copy-start.4 = (bf16[768,128]{1,0:T(8,128)(2,1)S(1)}, bf16[768,128]{1,0:T(8,128)(2,1)}, u32[]{:S(2)}) copy-start(bf16[768,128]{1,0:T(8,128)(2,1)} %get-tuple-element.8) | copy-start | bytes 589828
  126.8 2.6 %copy-start.5 = (f32[2,128]{1,0:T(2,128)S(1)}, f32[2,128]{1,0:T(2,128)}, u32[]{:S(2)}) copy-start(f32[2,128]{1,0:T(2,128)} %get-tuple-element.27) | copy-start | bytes 3076
where the time goes:
time: 130 us
  Pallas kernels  112 us (86%)
  local copies, waits for them, and re-layouts  17.5 us (13%)
    pallas_call x1, Pallas kernels, shards(): pl.pallas_call(functools.partial(body, (width, n_t, n_s)), out_shape=(jax...  112 us
    unnamed x21, local copies, waits for them, and re-layouts  9.32 us
    reshape x2, local copies, waits for them, and re-layouts, stacked(): return kernel.reshape(channels, 9, 3 * half).transpose(1, 0, 2)  4.49 us

commit v1 on v0

v1 whole, which is shorter than its diff:
```python
import functools

import jax
import jax.numpy as jnp
from jax import lax
from jax.experimental import pallas as pl
from jax.experimental.pallas import tpu as pltpu
from jax.sharding import PartitionSpec as P

GROUPS = 32
EPS = 1e-06
MESH = pl.DeviceIdType.MESH
F32 = jnp.float32
BF16 = jnp.bfloat16


def group_sums(values, per):
    channels = values.shape[1]
    row = lax.broadcasted_iota(jnp.int32, (channels, channels), 0) // per
    col = lax.broadcasted_iota(jnp.int32, (channels, channels), 1) // per
    same = jnp.where(row == col, 1.0, 0.0).astype(F32)
    return jnp.dot(values, same, precision=lax.Precision.HIGHEST, preferred_element_type=F32)


def body(
    sizes,
    f_ref, h_ref, cot_ref, k1_ref, k2_ref, gain_ref,
    fg_ref, d1_ref, d2_ref, w_ref,
    grads, taps, gh, kcat, turned, raw, act, acc, xs, xr, vec, r0, r2, r1, out, got, perm,
    k_sem, gx_s, gx_r, gz_s, gz_r, ge_s, ge_r, gr_s, gr_r, gg_s, gg_r,
    ai_s, ai_r, an_s, an_r, ad_s, ad_r, dl_s, dl_r, xsem_s, xsem_r, ar_s, ar_r,
):
    width, n_t, n_s, q = sizes
    frames, height, padded, channels = cot_ref.shape
    half = channels // 2
    per = channels // GROUPS
    n = n_t * n_s
    nj = n_t // q
    rows = frames * height * padded
    lanes = height * padded
    tall = n_s * height
    share = channels // n
    cs = channels // (q * n_s)
    hc = cs // 2
    t = lax.axis_index("tm")
    s = lax.axis_index("space")
    chan = lax.axis_index("chan")
    partner = 1 - chan
    rank = t * n_s + s
    r = lax.rem(t, q)
    p = t // q
    members = float(frames * height * width * per * n)
    mine = pl.ds(pl.multiple_of(chan * half, half), half)
    theirs = pl.ds(pl.multiple_of(partner * half, half), half)
    own_rows = pl.ds(s * height, height)
    own_frames = pl.ds(r * frames, frames)
    next_frames = pl.ds((r + 1) * frames, frames)
    sibling = {"chan": partner}

    def place(j):
        return {"tm": j // n_s, "space": lax.rem(j, n_s)}

    def peer(k):
        return lax.rem(rank + k, n)

    def each_peer(fn):
        def step(k, carry):
            fn(k)
            return carry

        lax.fori_loop(1, n, step, 0)

    def remote(src, dst, send, recv, device):
        return pltpu.make_async_remote_copy(
            src_ref=src, dst_ref=dst, send_sem=send, recv_sem=recv,
            device_id=device, device_id_type=MESH,
        )

    def kernel_copy(layer, source, c):
        return pltpu.make_async_copy(
            source.at[:, c], kcat.at[layer, :, :, c * half : (c + 1) * half], k_sem.at[layer, c]
        )

    for c in range(3):
        kernel_copy(0, k2_ref, c).start()
    for c in range(3):
        kernel_copy(1, k1_ref, c).start()

    barrier = pltpu.get_barrier_semaphore()
    pl.semaphore_signal(barrier, inc=1, device_id=sibling, device_id_type=MESH)
    each_peer(
        lambda k: pl.semaphore_signal(barrier, inc=1, device_id=place(peer(k)), device_id_type=MESH)
    )
    for layer in range(2):
        edge = jnp.zeros((q * frames + 2, 1, padded, 3 * half), BF16)
        taps[layer, :, 0:1] = edge
        taps[layer, :, tall + 1 : tall + 2] = edge

        @pl.when(t == n_t - 1)
        def _(layer=layer):
            def clear(f, carry):
                taps[layer, q * frames + f] = jnp.zeros((tall + 2, padded, 3 * half), BF16)
                return carry

            lax.fori_loop(0, 2, clear, 0)

    pl.semaphore_wait(barrier, n)

    def inside(value, count):
        return (value >= 0) & (value < count)

    def moves(layer, source):
        box = grads.at[layer]
        found = []
        before = jnp.where(r > 0, r, q) * frames
        sent = pl.ds(before, frames)

        def add(kind, go, src, dst, to, come, land, sender, send, recv):
            found.append((
                kind, go, lambda: remote(src, dst, send, recv, to),
                come, lambda: remote(land, land, send, recv, sender),
            ))

        for d, (ds, row) in enumerate(((1, height - 1), (-1, 0))):
            back = (s - ds) * height + row
            add(
                "near",
                (t > 0) & inside(s + ds, n_s),
                source.at[:, row : row + 1],
                box.at[sent, pl.ds(s * height + row, 1)],
                {"tm": t - 1, "space": s + ds},
                (t + 1 < n_t) & inside(s - ds, n_s),
                box.at[next_frames, pl.ds(back, 1)],
                {"tm": t + 1, "space": s - ds},
                ge_s.at[layer, d], ge_r.at[layer, d],
            )
        add(
            "near", t > 0, source, box.at[sent, own_rows], {"tm": t - 1},
            t + 1 < n_t, box.at[next_frames, own_rows], {"tm": t + 1},
            gz_s.at[layer], gz_r.at[layer],
        )
        for k in range(1, n_s):
            to, back = lax.rem(s + k, n_s), lax.rem(s + n_s - k, n_s)
            add(
                "near", None, source, box.at[own_frames, own_rows], {"space": to},
                None, box.at[own_frames, pl.ds(back * height, height)], {"space": back},
                gx_s.at[layer, k], gx_r.at[layer, k],
            )
        if q > 1:
            for k in sorted(range(1 - n_s, n_s), key=abs):
                i = k + n_s - 1
                earlier = pl.ds((r - 1) * frames, frames)
                add(
                    "side" if k == 0 else "far",
                    (r < q - 1) & inside(s + k, n_s),
                    source,
                    box.at[own_frames, own_rows],
                    {"tm": t + 1, "space": s + k},
                    (r > 0) & inside(s - k, n_s),
                    box.at[earlier, pl.ds((s - k) * height, height)],
                    {"tm": t - 1, "space": s - k},
                    gg_s.at[layer, i], gg_r.at[layer, i],
                )
                if k == 0:
                    continue
                low, count = (0, height) if abs(k) > 1 else ((0, height - 1) if k > 0 else (1, height - 1))
                add(
                    "far",
                    (r > 0) & inside(s + k, n_s),
                    source.at[:, low : low + count],
                    box.at[own_frames, pl.ds(s * height + low, count)],
                    {"tm": t - 1, "space": s + k},
                    (r < q - 1) & inside(s - k, n_s),
                    box.at[next_frames, pl.ds((s - k) * height + low, count)],
                    {"tm": t + 1, "space": s - k},
                    gr_s.at[layer, i], gr_r.at[layer, i],
                )
        return found

    def when(predicate, action):
        if predicate is None:
            action()
        else:
            pl.when(predicate)(action)

    def send_moves(found, kinds):
        for kind, go, copy, _, _ in found:
            if kind in kinds:
                when(go, lambda copy=copy: copy().start())

    def take_moves(found, kinds):
        for kind, _, _, come, copy in found:
            if kind in kinds:
                when(come, lambda copy=copy: copy().wait_recv())

    def end_moves(found):
        for _, go, copy, _, _ in found:
            when(go, lambda copy=copy: copy().wait_send())

    def set_rows(to_r, to_s):
        start = (to_r * n_s + to_s) * cs + chan * hc
        return pl.ds(pl.multiple_of(start, hc), hc)

    my_half = pl.ds(pl.multiple_of(chan * hc, hc), hc)

    def strip(at):
        return pl.ds(pl.multiple_of(at * lanes, lanes), lanes)

    def field_moves(layer):
        found = []
        for dr in range(q):
            for k in range(n_s):
                if dr == 0 and k == 0:
                    continue
                to_r, to_s = lax.rem(r + dr, q), lax.rem(s + k, n_s)
                from_r, from_s = lax.rem(r + q - dr, q), lax.rem(s + n_s - k, n_s)
                src = turned.at[layer, :, set_rows(to_r, to_s)]
                dst = raw.at[layer, pl.ds(2 + r * frames, frames), my_half, strip(s)]
                land = raw.at[layer, pl.ds(2 + from_r * frames, frames), my_half, strip(from_s)]
                sems = (ai_s.at[layer, dr, k], ai_r.at[layer, dr, k])
                found.append((
                    "in", None,
                    functools.partial(remote, src, dst, *sems, {"tm": p * q + to_r, "space": to_s}),
                    None,
                    functools.partial(remote, land, land, *sems, {"tm": p * q + from_r, "space": from_s}),
                ))
        for to_r in range(q):
            for k in range(n_s):
                to_s, from_s = lax.rem(s + k, n_s), lax.rem(s + n_s - k, n_s)
                src = turned.at[layer, frames - 2 : frames, set_rows(to_r, to_s)]
                dst = raw.at[layer, 0:2, my_half, strip(s)]
                land = raw.at[layer, 0:2, my_half, strip(from_s)]
                sems = (an_s.at[layer, to_r, k], an_r.at[layer, k])
                found.append((
                    "on", (r == q - 1) & (p + 1 < nj),
                    functools.partial(remote, src, dst, *sems, {"tm": (p + 1) * q + to_r, "space": to_s}),
                    (p > 0) if to_r == 0 else False,
                    functools.partial(remote, land, land, *sems, {"tm": p * q - 1, "space": from_s}),
                ))
        return found

    def take_fields(found):
        for _, _, _, come, copy in found:
            if come is not False:
                when(come, lambda copy=copy: copy().wait_recv())

    def across(layer):
        half_set = raw.at[layer, :, my_half]
        return remote(half_set, half_set, ad_s.at[layer], ad_r.at[layer], sibling)

    def across_land(layer):
        other = raw.at[layer, :, pl.ds(pl.multiple_of(partner * hc, hc), hc)]
        return remote(other, other, ad_s.at[layer], ad_r.at[layer], sibling)

    def sums_copy(layer, buf, k, slot):
        return remote(
            buf.at[slot], buf.at[slot], ar_s.at[layer, k], ar_r.at[layer, slot], place(peer(k))
        )

    def sums_start(layer, buf, values):
        buf[rank] = values
        each_peer(lambda k: sums_copy(layer, buf, k, rank).start())

    def sums_finish(layer, buf):
        each_peer(lambda k: sums_copy(layer, buf, k, peer(k)).wait_recv())
        return jnp.sum(buf[...], axis=0)

    def sums_end(layer, buf):
        each_peer(lambda k: sums_copy(layer, buf, k, rank).wait_send())

    def block_copy(layer, k, b):
        to = lax.rem(p + k, nj)
        return remote(
            out.at[layer, to, b], got.at[layer, k, b], dl_s.at[layer, k, b], dl_r.at[layer, k, b],
            {"tm": to * q + r},
        )

    def cross(layer):
        return remote(xs.at[layer], xr.at[layer], xsem_s.at[layer], xsem_r.at[layer], sibling)

    column = lax.rem(lax.broadcasted_iota(jnp.int32, (rows, 1), 0), padded)
    real = column < width

    def fill(layer, f, row, count):
        cells = grads[layer, f, pl.ds(row, count)].reshape(count * padded, half).astype(F32)
        size = count * padded
        ahead = pltpu.roll(cells, size - 1, 0)
        behind = pltpu.roll(cells, 1, 0)
        for c, value in enumerate((ahead, cells, behind)):
            taps[layer, f, pl.ds(row + 1, count), :, c * half : (c + 1) * half] = value.astype(
                BF16
            ).reshape(count, padded, half)

    def fill_frames(layer, first, strips):
        def step(i, carry):
            f, at = i // len(strips), lax.rem(i, len(strips))
            fill(layer, first + f, strips[0] * height if len(strips) == 1 else at * height, height)
            return carry

        lax.fori_loop(0, frames * len(strips), step, 0)

    def fill_near(layer):
        fill_frames(layer, r * frames, list(range(n_s)))

        @pl.when(t + 1 < n_t)
        def _():
            for f in range(frames):
                fill(layer, (r + 1) * frames + f, s * height, height)

        for row, ok in ((s * height - 1, s > 0), ((s + 1) * height, s + 1 < n_s)):
            @pl.when(ok & (t + 1 < n_t))
            def _(row=row):
                for f in range(frames):
                    fill(layer, (r + 1) * frames + f, row, 1)

    def fill_far(layer):
        for other in range(q):
            @pl.when(r != other)
            def _(other=other):
                fill_frames(layer, other * frames, list(range(n_s)))

    def conv(layer, source):
        for c in range(3):
            kernel_copy(layer, source, c).wait()
        for f in range(frames):
            total = None
            for ab in range(9):
                a, b = ab // 3, ab % 3
                left = taps[
                    layer, r * frames + (2 - a + f), pl.ds(s * height + (2 - b), height)
                ].reshape(lanes, 3 * half)
                term = lax.dot_general(
                    left, kcat[layer, ab], (((1,), (1,)), ((), ())), preferred_element_type=F32
                )
                total = term if total is None else total + term
            acc[f * lanes : (f + 1) * lanes] = total
        xs[layer] = acc[:, theirs].astype(BF16)
        cross(layer).start()

    def norm_back(field_ref, base, layer):
        cross(layer).wait_recv()
        upstream = acc[:, mine] + xr[layer].astype(F32)
        field = field_ref[:, :, :, mine].reshape(rows, half).astype(F32)
        scale = vec[base + 1 : base + 2, mine]
        gain = vec[base + 2 : base + 3, mine]
        centred = (field - vec[base : base + 1, mine]) * scale
        scaled = centred * gain
        gate = jax.nn.sigmoid(scaled)
        slope = jnp.where(real, upstream * gate * (1.0 + scaled * (1.0 - gate)), 0.0)
        acc[:, mine] = slope
        parts = [
            jnp.sum(slope, axis=0, keepdims=True),
            jnp.sum(slope * centred, axis=0, keepdims=True),
            jnp.zeros((6, half), F32),
        ]
        sums_start(layer + 1, (r2, r1)[layer], jnp.concatenate(parts, axis=0))

    def norm_end(field_ref, base, layer, w_row):
        totals = sums_finish(layer + 1, (r2, r1)[layer])
        w_ref[w_row : w_row + 1] = totals[1:2]
        scale = vec[base + 1 : base + 2, mine]
        gain = vec[base + 2 : base + 3, mine]
        means = group_sums(totals * gain, per) / members
        field = field_ref[:, :, :, mine].reshape(rows, half).astype(F32)
        centred = (field - vec[base : base + 1, mine]) * scale
        grad = scale * (acc[:, mine] * gain - means[0:1] - centred * means[1:2])
        return jnp.where(real, grad, 0.0)

    def turn(field_ref, layer):
        for f in range(frames):
            cells = field_ref[f].reshape(lanes, channels)
            flat = lax.dot_general(
                perm[...], cells, (((1,), (1,)), ((), ())), preferred_element_type=F32
            ).astype(BF16)
            turned[layer, f] = flat
        raw[layer, pl.ds(2 + r * frames, frames), my_half, strip(s)] = turned[layer, :, set_rows(r, s)]

    def activate(layer, base):
        pick = perm[pl.ds(pl.multiple_of((r * n_s + s) * cs, cs), cs)].astype(F32)
        cols = lax.dot_general(
            pick, vec[...], (((1,), (1,)), ((), ())),
            precision=lax.Precision.HIGHEST, preferred_element_type=F32,
        )
        mean, scale, gain = (cols[:, base + i : base + i + 1] for i in range(3))
        spot = lax.rem(lax.broadcasted_iota(jnp.int32, (1, tall * padded), 1), padded)

        def step(f, carry):
            field = raw[layer, f].astype(F32)
            scaled = (field - mean) * scale * gain
            keep = (spot < width) & ((f >= 2) | (p > 0))
            active = jnp.where(keep, scaled * jax.nn.sigmoid(scaled), 0.0)
            act[layer, f] = active.astype(BF16)
            return carry

        lax.fori_loop(0, q * frames + 2, step, 0)

    def delta(layer, own):
        for b in range(3):
            product = None
            for f in range(q * frames):
                left = act[layer, f : f + 3].reshape(3 * cs, tall * padded)
                right = taps[layer, f, 2 - b : 2 - b + tall].reshape(tall * padded, 3 * half)
                term = jnp.dot(left, right, preferred_element_type=F32)
                product = term if product is None else product + term
            small = product.astype(BF16)
            for j in range(nj):
                for a in range(3):
                    low = a * cs + j * share
                    out[layer, j, b, a] = small[low : low + share]

                @pl.when(p == j)
                def _(j=j):
                    for a in range(3):
                        low = a * cs + j * share
                        for c in range(3):
                            own[a * 9 + b * 3 + c] = product[
                                low : low + share, c * half : (c + 1) * half
                            ]

            for k in range(1, nj):
                block_copy(layer, k, b).start()

    moves_two = moves(0, cot_ref.at[:, :, :, mine])
    moves_one = moves(1, gh)
    send_moves(moves_two, ("near", "side"))
    grads[0, own_frames, own_rows] = cot_ref[:, :, :, mine]

    field_one = f_ref[...].reshape(rows, channels).astype(F32)
    field_two = h_ref[...].reshape(rows, channels).astype(F32)
    parts = [
        jnp.sum(field_one, axis=0, keepdims=True),
        jnp.sum(field_one * field_one, axis=0, keepdims=True),
        jnp.sum(field_two, axis=0, keepdims=True),
        jnp.sum(field_two * field_two, axis=0, keepdims=True),
        jnp.zeros((4, channels), F32),
    ]
    sums_start(0, r0, jnp.concatenate(parts, axis=0))

    place_row = lax.broadcasted_iota(jnp.int32, (channels, channels), 0)
    place_col = lax.broadcasted_iota(jnp.int32, (channels, channels), 1)
    element = lax.rem(place_row, share)
    block = lax.rem(place_row // share, nj)
    which = place_row // (share * nj)
    wanted = ((block * q + which // n_s) * n_s + lax.rem(which, n_s)) * share + element
    perm[...] = jnp.where(place_col == wanted, 1.0, 0.0).astype(BF16)

    fields_two = field_moves(0)
    fields_one = field_moves(1)
    turn(h_ref, 0)
    for _, go, copy, _, _ in fields_two:
        when(go, lambda copy=copy: copy().start())
    turn(f_ref, 1)
    for _, go, copy, _, _ in fields_one:
        when(go, lambda copy=copy: copy().start())

    take_moves(moves_two, ("near",))
    fill_near(0)
    conv(0, k2_ref)

    totals = group_sums(sums_finish(0, r0), per) / members
    mean_one, mean_two = totals[0:1], totals[2:3]
    vec[0:1] = mean_one
    vec[1:2] = lax.rsqrt(totals[1:2] - mean_one * mean_one + EPS)
    vec[2:3] = gain_ref[0:1]
    vec[3:4] = mean_two
    vec[4:5] = lax.rsqrt(totals[3:4] - mean_two * mean_two + EPS)
    vec[5:6] = gain_ref[1:2]
    vec[6:8] = jnp.zeros((2, channels), F32)

    norm_back(h_ref, 3, 0)
    send_moves(moves_two, ("far",))
    take_fields(fields_two)
    across(0).start()
    gh[...] = norm_end(h_ref, 3, 0, 1).astype(BF16).reshape(frames, height, padded, half)
    send_moves(moves_one, ("near", "side"))
    send_moves(moves_one, ("far",))
    grads[1, own_frames, own_rows] = gh[...]

    across_land(0).wait_recv()
    activate(0, 3)
    take_moves(moves_two, ("side", "far"))
    fill_far(0)
    delta(0, d2_ref)
    take_fields(fields_one)
    across(1).start()

    take_moves(moves_one, ("near",))
    fill_near(1)
    conv(1, k1_ref)
    across_land(1).wait_recv()
    activate(1, 0)
    norm_back(f_ref, 0, 1)
    take_moves(moves_one, ("side", "far"))
    fill_far(1)
    delta(1, d1_ref)
    grad = norm_end(f_ref, 0, 1, 0)
    fg_ref[...] = (cot_ref[:, :, :, mine].reshape(rows, half).astype(F32) + grad).astype(BF16)

    for layer, own in ((0, d2_ref), (1, d1_ref)):
        for k in range(1, nj):
            for b in range(3):
                block_copy(layer, k, b).wait_recv()
                for a in range(3):
                    more = got[layer, k, b, a].astype(F32)
                    for c in range(3):
                        own[a * 9 + b * 3 + c] += more[:, c * half : (c + 1) * half]

    end_moves(moves_two)
    end_moves(moves_one)
    for found in (fields_two, fields_one):
        for _, go, copy, _, _ in found:
            when(go, lambda copy=copy: copy().wait_send())
    sums_end(0, r0)
    sums_end(1, r2)
    sums_end(2, r1)
    for layer in range(2):
        cross(layer).wait_send()
        across(layer).wait_send()
        for k in range(1, nj):
            for b in range(3):
                block_copy(layer, k, b).wait_send()


def shards(n_t, n_s, features, hidden, cotangent, kernel_one, kernel_two, gains):
    frames, height, width, channels = features.shape
    half = kernel_one.shape[4]
    padded = -(-width // 16) * 16
    if padded < width + 1:
        padded += 16
    q = 2 if n_t % 2 == 0 else 1
    n = n_t * n_s
    nj = n_t // q
    share = channels // n
    cs = channels // (q * n_s)
    rows = frames * height * padded
    lanes = height * padded
    tall = n_s * height

    def wide(field):
        return jnp.pad(field, ((0, 0), (0, 0), (0, padded - width), (0, 0)))

    def stacked(kernel):
        return kernel.transpose(1, 2, 3, 0, 4).reshape(9, 3, channels, half)

    vmem = pl.BlockSpec(memory_space=pltpu.VMEM)
    hbm = pl.BlockSpec(memory_space=pl.ANY)
    dma = pltpu.SemaphoreType.DMA
    around = 2 * n_s - 1
    grad, delta_one, delta_two, weighted = pl.pallas_call(
        functools.partial(body, (width, n_t, n_s, q)),
        out_shape=(
            jax.ShapeDtypeStruct((rows, half), BF16),
            jax.ShapeDtypeStruct((27, share, half), F32),
            jax.ShapeDtypeStruct((27, share, half), F32),
            jax.ShapeDtypeStruct((2, half), F32),
        ),
        in_specs=[vmem, vmem, vmem, hbm, hbm, vmem],
        out_specs=(vmem,) * 4,
        scratch_shapes=[
            pltpu.VMEM((2, q * frames + 2, tall, padded, half), BF16),
            pltpu.VMEM((2, q * frames + 2, tall + 2, padded, 3 * half), BF16),
            pltpu.VMEM((frames, height, padded, half), BF16),
            pltpu.VMEM((2, 9, channels, 3 * half), BF16),
            pltpu.VMEM((2, frames, channels, lanes), BF16),
            pltpu.VMEM((2, q * frames + 2, cs, tall * padded), BF16),
            pltpu.VMEM((2, q * frames + 2, cs, tall * padded), BF16),
            pltpu.VMEM((rows, channels), F32),
            pltpu.VMEM((2, rows, half), BF16),
            pltpu.VMEM((2, rows, half), BF16),
            pltpu.VMEM((8, channels), F32),
            pltpu.VMEM((n, 8, channels), F32),
            pltpu.VMEM((n, 8, half), F32),
            pltpu.VMEM((n, 8, half), F32),
            pltpu.VMEM((2, nj, 3, 3, share, 3 * half), BF16),
            pltpu.VMEM((2, nj, 3, 3, share, 3 * half), BF16),
            pltpu.VMEM((channels, channels), BF16),
            dma((2, 3)),
            dma((2, n_s)), dma((2, n_s)),
            dma((2,)), dma((2,)),
            dma((2, 2)), dma((2, 2)),
            dma((2, around)), dma((2, around)),
            dma((2, around)), dma((2, around)),
            dma((2, q, n_s)), dma((2, q, n_s)),
            dma((2, q, n_s)), dma((2, n_s)),
            dma((2,)), dma((2,)),
            dma((2, nj, 3)), dma((2, nj, 3)),
            dma((2,)), dma((2,)),
            dma((3, n)), dma((3, n)),
        ],
        compiler_params=pltpu.CompilerParams(
            collective_id=0, has_side_effects=True, vmem_limit_bytes=63 * 1024 * 1024
        ),
    )(wide(features), wide(hidden), wide(cotangent), stacked(kernel_one), stacked(kernel_two), gains)

    def unstacked(delta):
        return delta.reshape(3, 3, 3, share, half).transpose(3, 0, 1, 2, 4)

    feature_grad = grad.reshape(frames, height, padded, half)[:, :, :width]
    return (feature_grad, unstacked(delta_one), unstacked(delta_two), weighted)


def solution(mesh):
    placed = (
        P(("clip", "tm"), "space", None, None),
        P(("clip", "tm"), "space", None, None),
        P(("clip", "tm"), "space", None, None),
        P(None, None, None, None, "chan"),
        P(None, None, None, None, "chan"),
        P(),
    )
    return jax.shard_map(
        functools.partial(shards, mesh.shape["tm"], mesh.shape["space"]),
        mesh=mesh,
        in_specs=placed,
        out_specs=(
            P(("clip", "tm"), "space", None, "chan"),
            P(("clip", "tm", "space"), None, None, None, "chan"),
            P(("clip", "tm", "space"), None, None, None, "chan"),
            P("clip", "chan"),
        ),
        check_vma=False,
    )
```

time: 130 us -> 64 us (0.49)
  Pallas kernels: 112 us -> 53.7 us
  local copies, waits for them, and re-layouts: 17.5 us -> 9.42 us
    pallas_call x1, Pallas kernels: 112 us -> 53.7 us  [shards(): pl.pallas_call(functools.partial(body, (width, n_t, n_s, q)), out_shape=(...]
    reshape x4 -> x0, local copies, waits for them, and re-layouts: 5.9 us -> none  [the longest x2 4.49 us: stacked(): return kernel.reshape(channels, 9, 3 * half).transpose(1, 0, 2)]
    unnamed x21 -> x13, local copies, waits for them, and re-layouts: 9.32 us -> 7.06 us
where the time goes in v1:
time: 64 us; the launch traced here: 63.8 us
  Pallas kernels  53.7 us (84%)
  local copies, waits for them, and re-layouts  9.42 us (15%)
  between operations  0.68 us (1%)
    pallas_call x1, Pallas kernels, shards(): pl.pallas_call(functools.partial(body, (width, n_t, n_s, q)), out_shape=(...  53.7 us
    unnamed x13, local copies, waits for them, and re-layouts  7.06 us
    pad x3, local copies, waits for them, and re-layouts, wide(): return jnp.pad(field, ((0, 0), (0, 0), (0, padded - width), (0, 0)))  2.35 us

profile of v1, /device:TPU:0, one launch (start us, length us, event | category | flops | bytes accessed | tf_op | source)
XLA Modules:
  0.0 63.8 jit_solution(8775238247622531943)
XLA Ops:
  0.6 0.0 copy-start.1
  0.6 0.0 copy-start
  0.7 1.1 %copy.10 = bf16[2,4,90,256]{3,2,1,0:T(8,128)(2,1)S(1)} copy(bf16[2,4,90,256]{3,1,2,0:T(4,128)(2,1)} %param.6) | data formatting | bytes 737280 | tf_op args[0]
  1.8 0.8 %pad.10.f_ref = bf16[2,4,96,256]{3,2,1,0:T(8,128)(2,1)} pad(bf16[2,4,90,256]{3,2,1,0:T(8,128)(2,1)S(1)} %copy.10, bf16[]{:T(256)} %constant.2.clone.1), padding=0_0x0_0x0_6x0_0 | pad | bytes 761858 | tf_op jit(solution)/shard_map/jit(_pad)/pad | solution.py:540
  2.5 0.0 copy-done
  2.6 0.8 %pad.11.h_ref = bf16[2,4,96,256]{3,2,1,0:T(8,128)(2,1)} pad(bf16[2,4,90,256]{3,2,1,0:T(8,128)(2,1)S(1)} %copy.11, bf16[]{:T(256)} %constant.2.clone.1), padding=0_0x0_0x0_6x0_0 | pad | bytes 761858 | tf_op jit(solution)/shard_map/jit(_pad)/pad | solution.py:540
  3.4 0.0 copy-done.1
  3.4 0.8 %pad.12.cot_ref = bf16[2,4,96,256]{3,2,1,0:T(8,128)(2,1)} pad(bf16[2,4,90,256]{3,2,1,0:T(8,128)(2,1)S(1)} %copy.12, bf16[]{:T(256)} %constant.2.clone.1), padding=0_0x0_0x0_6x0_0 | pad | bytes 761858 | tf_op jit(solution)/shard_map/jit(_pad)/pad | solution.py:540
  4.2 53.7 %shard_map.93 = (bf16[768,128]{1,0:T(8,128)(2,1)}, f32[27,32,128]{2,1,0:T(8,128)}, f32[27,32,128]{2,1,0:T(8,128)}, f32[2,128]{1,0:T(2,128)}) custom-call(bf16[2,4,96,256]{3,2,1,0:T(8,128)(2,1)} %pad.10.f_ref, bf16[2,4,96,256]{3,2,1,0:T(8,128)(2,1)} %pad.11.h_ref, bf16[2,4,96,256]{3,2,1,0:T(8,128)(2,1)} %pad.12.cot_ref, bf16[9,3,256,128]{3,2,1,0:T(8,128)(2,1)} %bitcast.14, ...), custom_call_target="tpu_custom_call" | custom-call | tf_op jit(solution)/shard_map/pallas_call | solution.py:549
  57.9 0.0 copy-start.2
  57.9 1.7 %copy.14 = bf16[2,4,90,128]{3,1,2,0:T(4,128)(2,1)} copy(bf16[2,4,90,128]{3,2,1,0:T(8,128)(2,1)} %bitcast.18) | data formatting | bytes 368640
  59.6 1.8 %copy.18 = f32[32,3,3,3,128]{4,0,3,2,1:T(8,128)} copy(f32[32,3,3,3,128]{4,0,3,2,1:T(8,128)} %bitcast.17) | data formatting | bytes 884736
  61.4 1.8 %copy.19 = f32[32,3,3,3,128]{4,0,3,2,1:T(8,128)} copy(f32[32,3,3,3,128]{4,0,3,2,1:T(8,128)} %bitcast.16) | data formatting | bytes 884736
  63.2 0.0 copy-done.2
  63.2 0.6 copy.20
  (2 shorter events, 0.1 us)
Async XLA Ops:
  0.6 2.7 %copy-start.1 = (bf16[2,4,90,256]{3,1,2,0:T(4,128)(2,1)S(1)}, bf16[2,4,90,256]{3,1,2,0:T(4,128)(2,1)}, u32[]{:S(2)}) copy-start(bf16[2,4,90,256]{3,1,2,0:T(4,128)(2,1)} %param.8) | copy-start | bytes 1105924
  0.6 1.9 %copy-start = (bf16[2,4,90,256]{3,1,2,0:T(4,128)(2,1)S(1)}, bf16[2,4,90,256]{3,1,2,0:T(4,128)(2,1)}, u32[]{:S(2)}) copy-start(bf16[2,4,90,256]{3,1,2,0:T(4,128)(2,1)} %param.7) | copy-start | bytes 1105924
  57.9 5.3 %copy-start.2 = (f32[2,128]{1,0:T(2,128)S(1)}, f32[2,128]{1,0:T(2,128)}, u32[]{:S(2)}) copy-start(f32[2,128]{1,0:T(2,128)} %get-tuple-element.19) | copy-start | bytes 3076

commit v2 on v1

--- a/solution.py
+++ b/solution.py
@@ -26,7 +26,7 @@
     sizes,
     f_ref, h_ref, cot_ref, k1_ref, k2_ref, gain_ref,
     fg_ref, d1_ref, d2_ref, w_ref,
-    grads, taps, gh, kcat, turned, raw, act, acc, xs, xr, vec, r0, r2, r1, out, got, perm,
+    grads, hop, taps, gh, kcat, turned, raw, act, acc, xs, xr, vec, r0, r2, r1, out, got, perm,
     k_sem, gx_s, gx_r, gz_s, gz_r, ge_s, ge_r, gr_s, gr_r, gg_s, gg_r,
     ai_s, ai_r, an_s, an_r, ad_s, ad_r, dl_s, dl_r, xsem_s, xsem_r, ar_s, ar_r,
 ):
@@ -55,6 +55,7 @@
     own_rows = pl.ds(s * height, height)
     own_frames = pl.ds(r * frames, frames)
     next_frames = pl.ds((r + 1) * frames, frames)
+    mate_frames = pl.ds((q - 1 - r) * frames, frames)
     sibling = {"chan": partner}
 
     def place(j):
@@ -139,41 +140,34 @@
             t + 1 < n_t, box.at[next_frames, own_rows], {"tm": t + 1},
             gz_s.at[layer], gz_r.at[layer],
         )
-        for k in range(1, n_s):
-            to, back = lax.rem(s + k, n_s), lax.rem(s + n_s - k, n_s)
+        for k in sorted((k for k in range(1 - n_s, n_s) if k), key=abs):
+            i = k + n_s - 1
+            spans = (("wide", 0, height),)
+            if abs(k) == 1:
+                spans = (("near x", height - 1, 1), ("wide", 0, height - 1))
+                if k < 0:
+                    spans = (("near x", 0, 1), ("wide", 1, height - 1))
+            for part, (kind, low, count) in enumerate(spans):
+                add(
+                    kind, inside(s + k, n_s), source.at[:, low : low + count],
+                    box.at[own_frames, pl.ds(s * height + low, count)], {"space": s + k},
+                    inside(s - k, n_s),
+                    box.at[own_frames, pl.ds((s - k) * height + low, count)], {"space": s - k},
+                    gx_s.at[layer, part, i], gx_r.at[layer, part, i],
+                )
+        if q > 1:
+            earlier = pl.ds((r - 1) * frames, frames)
             add(
-                "near", None, source, box.at[own_frames, own_rows], {"space": to},
-                None, box.at[own_frames, pl.ds(back * height, height)], {"space": back},
-                gx_s.at[layer, k], gx_r.at[layer, k],
+                "side", r < q - 1, source, box.at[own_frames, own_rows], {"tm": t + 1},
+                r > 0, box.at[earlier, own_rows], {"tm": t - 1},
+                gg_s.at[layer], gg_r.at[layer],
             )
-        if q > 1:
-            for k in sorted(range(1 - n_s, n_s), key=abs):
-                i = k + n_s - 1
-                earlier = pl.ds((r - 1) * frames, frames)
+            for k in range(1, n_s):
+                to, back = lax.rem(s + k, n_s), lax.rem(s + n_s - k, n_s)
                 add(
-                    "side" if k == 0 else "far",
-                    (r < q - 1) & inside(s + k, n_s),
-                    source,
-                    box.at[own_frames, own_rows],
-                    {"tm": t + 1, "space": s + k},
-                    (r > 0) & inside(s - k, n_s),
-                    box.at[earlier, pl.ds((s - k) * height, height)],
-                    {"tm": t - 1, "space": s - k},
-                    gg_s.at[layer, i], gg_r.at[layer, i],
-                )
-                if k == 0:
-                    continue
-                low, count = (0, height) if abs(k) > 1 else ((0, height - 1) if k > 0 else (1, height - 1))
-                add(
-                    "far",
-                    (r > 0) & inside(s + k, n_s),
-                    source.at[:, low : low + count],
-                    box.at[own_frames, pl.ds(s * height + low, count)],
-                    {"tm": t - 1, "space": s + k},
-                    (r < q - 1) & inside(s - k, n_s),
-                    box.at[next_frames, pl.ds((s - k) * height + low, count)],
-                    {"tm": t + 1, "space": s - k},
-                    gr_s.at[layer, i], gr_r.at[layer, i],
+                    "relay", None, box.at[mate_frames, own_rows], hop.at[layer, k], {"space": to},
+                    None, hop.at[layer, k], {"space": back},
+                    gr_s.at[layer, k], gr_r.at[layer, k],
                 )
         return found
 
@@ -281,8 +275,9 @@
     column = lax.rem(lax.broadcasted_iota(jnp.int32, (rows, 1), 0), padded)
     real = column < width
 
-    def fill(layer, f, row, count):
-        cells = grads[layer, f, pl.ds(row, count)].reshape(count * padded, half).astype(F32)
+    def spread(layer, f, row, source):
+        count = source.shape[0]
+        cells = source.reshape(count * padded, half).astype(F32)
         size = count * padded
         ahead = pltpu.roll(cells, size - 1, 0)
         behind = pltpu.roll(cells, 1, 0)
@@ -291,41 +286,42 @@
                 BF16
             ).reshape(count, padded, half)
 
-    def fill_frames(layer, first, strips):
-        def step(i, carry):
-            f, at = i // len(strips), lax.rem(i, len(strips))
-            fill(layer, first + f, strips[0] * height if len(strips) == 1 else at * height, height)
-            return carry
-
-        lax.fori_loop(0, frames * len(strips), step, 0)
-
-    def fill_near(layer):
-        fill_frames(layer, r * frames, list(range(n_s)))
-
-        @pl.when(t + 1 < n_t)
-        def _():
-            for f in range(frames):
-                fill(layer, (r + 1) * frames + f, s * height, height)
-
+    def fill(layer, f, row, count):
+        spread(layer, f, row, grads[layer, f, pl.ds(row, count)])
+
+    def fill_rows(layer, first):
+        for f in range(frames):
+            fill(layer, first + f, s * height, height)
         for row, ok in ((s * height - 1, s > 0), ((s + 1) * height, s + 1 < n_s)):
-            @pl.when(ok & (t + 1 < n_t))
+            @pl.when(ok)
             def _(row=row):
                 for f in range(frames):
-                    fill(layer, (r + 1) * frames + f, row, 1)
-
-    def fill_far(layer):
-        for other in range(q):
-            @pl.when(r != other)
-            def _(other=other):
-                fill_frames(layer, other * frames, list(range(n_s)))
-
-    def conv(layer, source):
-        for c in range(3):
-            kernel_copy(layer, source, c).wait()
+                    fill(layer, first + f, row, 1)
+
+    def fill_rest(layer):
+        for k in range(1, n_s):
+            back = lax.rem(s + n_s - k, n_s)
+            for f in range(frames):
+                fill(layer, r * frames + f, back * height, height)
+                if q > 1:
+                    mate = (q - 1 - r) * frames + f
+                    spread(layer, mate, back * height, hop[layer, k, f])
+        if q > 1:
+            @pl.when(r > 0)
+            def _():
+                for f in range(frames):
+                    fill(layer, f, s * height, height)
+
+    def conv(layer, source, near):
+        if near:
+            for c in range(3):
+                kernel_copy(layer, source, c).wait()
         for f in range(frames):
             total = None
             for ab in range(9):
                 a, b = ab // 3, ab % 3
+                if (2 - a + f < frames) != near:
+                    continue
                 left = taps[
                     layer, r * frames + (2 - a + f), pl.ds(s * height + (2 - b), height)
                 ].reshape(lanes, 3 * half)
@@ -333,9 +329,15 @@
                     left, kcat[layer, ab], (((1,), (1,)), ((), ())), preferred_element_type=F32
                 )
                 total = term if total is None else total + term
-            acc[f * lanes : (f + 1) * lanes] = total
-        xs[layer] = acc[:, theirs].astype(BF16)
-        cross(layer).start()
+            if total is None:
+                continue
+            if near:
+                acc[f * lanes : (f + 1) * lanes] = total
+            else:
+                acc[f * lanes : (f + 1) * lanes] += total
+        if not near:
+            xs[layer] = acc[:, theirs].astype(BF16)
+            cross(layer).start()
 
     def norm_back(field_ref, base, layer):
         cross(layer).wait_recv()
@@ -422,7 +424,8 @@
 
     moves_two = moves(0, cot_ref.at[:, :, :, mine])
     moves_one = moves(1, gh)
-    send_moves(moves_two, ("near", "side"))
+    send_moves(moves_two, ("near x", "near"))
+    send_moves(moves_two, ("side", "wide"))
     grads[0, own_frames, own_rows] = cot_ref[:, :, :, mine]
 
     field_one = f_ref[...].reshape(rows, channels).astype(F32)
@@ -446,16 +449,22 @@
 
     fields_two = field_moves(0)
     fields_one = field_moves(1)
+
+    def send_fields(found):
+        for _, go, copy, _, _ in found:
+            when(go, lambda copy=copy: copy().start())
+
     turn(h_ref, 0)
-    for _, go, copy, _, _ in fields_two:
-        when(go, lambda copy=copy: copy().start())
+    send_fields(fields_two)
     turn(f_ref, 1)
-    for _, go, copy, _, _ in fields_one:
-        when(go, lambda copy=copy: copy().start())
-
-    take_moves(moves_two, ("near",))
-    fill_near(0)
-    conv(0, k2_ref)
+
+    take_moves(moves_two, ("near x",))
+    fill_rows(0, r * frames)
+    conv(0, k2_ref, True)
+    take_moves(moves_two, ("near", "side"))
+    send_moves(moves_two, ("relay",))
+    pl.when(t + 1 < n_t)(lambda: fill_rows(0, (r + 1) * frames))
+    conv(0, k2_ref, False)
 
     totals = group_sums(sums_finish(0, r0), per) / members
     mean_one, mean_two = totals[0:1], totals[2:3]
@@ -468,30 +477,34 @@
     vec[6:8] = jnp.zeros((2, channels), F32)
 
     norm_back(h_ref, 3, 0)
-    send_moves(moves_two, ("far",))
+    send_fields(fields_one)
     take_fields(fields_two)
     across(0).start()
-    gh[...] = norm_end(h_ref, 3, 0, 1).astype(BF16).reshape(frames, height, padded, half)
-    send_moves(moves_one, ("near", "side"))
-    send_moves(moves_one, ("far",))
-    grads[1, own_frames, own_rows] = gh[...]
-
+    take_moves(moves_two, ("wide", "relay"))
+    fill_rest(0)
     across_land(0).wait_recv()
     activate(0, 3)
-    take_moves(moves_two, ("side", "far"))
-    fill_far(0)
+    gh[...] = norm_end(h_ref, 3, 0, 1).astype(BF16).reshape(frames, height, padded, half)
+    send_moves(moves_one, ("near x", "near"))
+    send_moves(moves_one, ("side", "wide"))
+    grads[1, own_frames, own_rows] = gh[...]
+
     delta(0, d2_ref)
     take_fields(fields_one)
     across(1).start()
-
-    take_moves(moves_one, ("near",))
-    fill_near(1)
-    conv(1, k1_ref)
     across_land(1).wait_recv()
     activate(1, 0)
+
+    take_moves(moves_one, ("near x",))
+    fill_rows(1, r * frames)
+    conv(1, k1_ref, True)
+    take_moves(moves_one, ("near", "side"))
+    send_moves(moves_one, ("relay",))
+    pl.when(t + 1 < n_t)(lambda: fill_rows(1, (r + 1) * frames))
+    conv(1, k1_ref, False)
     norm_back(f_ref, 0, 1)
-    take_moves(moves_one, ("side", "far"))
-    fill_far(1)
+    take_moves(moves_one, ("wide", "relay"))
+    fill_rest(1)
     delta(1, d1_ref)
     grad = norm_end(f_ref, 0, 1, 0)
     fg_ref[...] = (cot_ref[:, :, :, mine].reshape(rows, half).astype(F32) + grad).astype(BF16)
@@ -558,6 +571,7 @@
         out_specs=(vmem,) * 4,
         scratch_shapes=[
             pltpu.VMEM((2, q * frames + 2, tall, padded, half), BF16),
+            pltpu.VMEM((2, n_s, frames, height, padded, half), BF16),
             pltpu.VMEM((2, q * frames + 2, tall + 2, padded, 3 * half), BF16),
             pltpu.VMEM((frames, height, padded, half), BF16),
             pltpu.VMEM((2, 9, channels, 3 * half), BF16),
@@ -575,11 +589,11 @@
             pltpu.VMEM((2, nj, 3, 3, share, 3 * half), BF16),
             pltpu.VMEM((channels, channels), BF16),
             dma((2, 3)),
+            dma((2, 2, around)), dma((2, 2, around)),
+            dma((2,)), dma((2,)),
+            dma((2, 2)), dma((2, 2)),
             dma((2, n_s)), dma((2, n_s)),
             dma((2,)), dma((2,)),
-            dma((2, 2)), dma((2, 2)),
-            dma((2, around)), dma((2, around)),
-            dma((2, around)), dma((2, around)),
             dma((2, q, n_s)), dma((2, q, n_s)),
             dma((2, q, n_s)), dma((2, n_s)),
             dma((2,)), dma((2,)),
@@ -588,7 +602,7 @@
             dma((3, n)), dma((3, n)),
         ],
         compiler_params=pltpu.CompilerParams(
-            collective_id=0, has_side_effects=True, vmem_limit_bytes=63 * 1024 * 1024
+            collective_id=0, has_side_effects=True, vmem_limit_bytes=40 * 1024 * 1024
         ),
     )(wide(features), wide(hidden), wide(cotangent), stacked(kernel_one), stacked(kernel_two), gains)
 

time: 64 us -> 57.4 us (0.90)
  local copies, waits for them, and re-layouts: 9.42 us -> 5.91 us
  Pallas kernels: 53.7 us -> 50.6 us
    pallas_call x1, Pallas kernels: 53.7 us -> 50.6 us  [shards(): pl.pallas_call(functools.partial(body, (width, n_t, n_s, q)), out_shape=(...]
    pad x3, local copies, waits for them, and re-layouts: 2.35 us -> 0.1 us  [wide(): return jnp.pad(field, ((0, 0), (0, 0), (0, padded - width), (0, 0)))]
    unnamed x13 -> x17, local copies, waits for them, and re-layouts: 7.06 us -> 5.81 us
where the time goes in v2:
time: 57.4 us; the launch traced here: 57.3 us
  Pallas kernels  50.6 us (88%)
  local copies, waits for them, and re-layouts  5.91 us (10%)
  between operations  0.74 us (1%)
    pallas_call x1, Pallas kernels, shards(): pl.pallas_call(functools.partial(body, (width, n_t, n_s, q)), out_shape=(...  50.6 us
    unnamed x17, local copies, waits for them, and re-layouts  5.81 us

profile of v2, /device:TPU:0, one launch (start us, length us, event | category | flops | bytes accessed | tf_op | source)
XLA Modules:
  0.0 57.3 jit_solution(11144135680709009722)
XLA Ops:
  0.6 0.0 copy-start.4
  0.6 0.0 copy-start.3
  0.7 1.1 %copy.10 = bf16[2,4,90,256]{3,2,1,0:T(8,128)(2,1)S(1)} copy(bf16[2,4,90,256]{3,1,2,0:T(4,128)(2,1)} %param.6) | data formatting | bytes 737280 | tf_op args[0]
  1.8 0.0 copy-start
  1.8 0.0 copy-start.1
  1.8 0.0 copy-start.2
  1.8 0.0 copy-done.3
  1.9 0.0 copy-done.4
  2.0 1.2 %copy-done = bf16[256,3,3,3,128]{4,0,3,2,1:T(8,128)(2,1)S(1)} copy-done((bf16[256,3,3,3,128]{4,0,3,2,1:T(8,128)(2,1)S(1)}, bf16[256,3,3,3,128]{4,0,3,2,1:T(8,128)(2,1)}, u32[]{:S(2)}) %copy-start) | copy-done | bytes 1769496
  3.3 0.5 copy-done.1
  3.8 0.0 copy-done.2
  3.8 50.6 %shard_map.93 = (bf16[768,128]{1,0:T(8,128)(2,1)S(1)}, f32[27,32,128]{2,1,0:T(8,128)S(1)}, f32[27,32,128]{2,1,0:T(8,128)S(1)}, f32[2,128]{1,0:T(2,128)S(1)}) custom-call(bf16[2,4,96,256]{3,2,1,0:T(8,128)(2,1)S(1)} %pad.10.f_ref, bf16[2,4,96,256]{3,2,1,0:T(8,128)(2,1)S(1)} %pad.11.h_ref, bf16[2,4,96,256]{3,2,1,0:T(8,128)(2,1)S(1)} %pad.12.cot_ref, ...), custom_call_target="tpu_custom_call" | custom-call | tf_op jit(solution)/shard_map/pallas_call | solution.py:562
  54.4 0.8 %copy.14 = bf16[2,4,90,128]{3,1,2,0:T(4,128)(2,1)} copy(bf16[2,4,90,128]{3,2,1,0:T(8,128)(2,1)S(1)} %bitcast.18) | data formatting | bytes 368640
  55.2 0.8 %copy.18 = f32[32,3,3,3,128]{4,0,3,2,1:T(8,128)} copy(f32[32,3,3,3,128]{4,0,3,2,1:T(8,128)S(1)} %bitcast.17) | data formatting | bytes 884736
  55.9 0.8 %copy.19 = f32[32,3,3,3,128]{4,0,3,2,1:T(8,128)} copy(f32[32,3,3,3,128]{4,0,3,2,1:T(8,128)S(1)} %bitcast.16) | data formatting | bytes 884736
  56.7 0.6 copy.20
  (5 shorter events, 0.2 us)
Async XLA Ops:
  0.6 1.3 %copy-start.4 = (bf16[2,4,90,256]{3,1,2,0:T(4,128)(2,1)S(1)}, bf16[2,4,90,256]{3,1,2,0:T(4,128)(2,1)}, u32[]{:S(2)}) copy-start(bf16[2,4,90,256]{3,1,2,0:T(4,128)(2,1)} %param.8) | copy-start | bytes 1105924
  0.6 1.2 %copy-start.3 = (bf16[2,4,90,256]{3,1,2,0:T(4,128)(2,1)S(1)}, bf16[2,4,90,256]{3,1,2,0:T(4,128)(2,1)}, u32[]{:S(2)}) copy-start(bf16[2,4,90,256]{3,1,2,0:T(4,128)(2,1)} %param.7) | copy-start | bytes 1105924
  1.8 1.5 %copy-start = (bf16[256,3,3,3,128]{4,0,3,2,1:T(8,128)(2,1)S(1)}, bf16[256,3,3,3,128]{4,0,3,2,1:T(8,128)(2,1)}, u32[]{:S(2)}) copy-start(bf16[256,3,3,3,128]{4,0,3,2,1:T(8,128)(2,1)} %param.9) | copy-start | bytes 5308420
  1.8 2.0 %copy-start.1 = (bf16[256,3,3,3,128]{4,0,3,2,1:T(8,128)(2,1)S(1)}, bf16[256,3,3,3,128]{4,0,3,2,1:T(8,128)(2,1)}, u32[]{:S(2)}) copy-start(bf16[256,3,3,3,128]{4,0,3,2,1:T(8,128)(2,1)} %param.10) | copy-start | bytes 5308420
  1.8 2.0 %copy-start.2 = (f32[2,256]{1,0:T(2,128)S(1)}, f32[2,256]{1,0:T(2,128)}, u32[]{:S(2)}) copy-start(f32[2,256]{1,0:T(2,128)} %gain_ref.1) | copy-start | bytes 6148

commit v3 on v2

--- a/solution.py
+++ b/solution.py
@@ -26,6 +26,7 @@
     sizes,
     f_ref, h_ref, cot_ref, k1_ref, k2_ref, gain_ref,
     fg_ref, d1_ref, d2_ref, w_ref,
+    fg, mixed, d1, d2, weights, o_sem,
     grads, hop, taps, gh, kcat, turned, raw, act, acc, xs, xr, vec, r0, r2, r1, out, got, perm,
     k_sem, gx_s, gx_r, gz_s, gz_r, ge_s, ge_r, gr_s, gr_r, gg_s, gg_r,
     ai_s, ai_r, an_s, an_r, ad_s, ad_r, dl_s, dl_r, xsem_s, xsem_r, ar_s, ar_r,
@@ -55,7 +56,6 @@
     own_rows = pl.ds(s * height, height)
     own_frames = pl.ds(r * frames, frames)
     next_frames = pl.ds((r + 1) * frames, frames)
-    mate_frames = pl.ds((q - 1 - r) * frames, frames)
     sibling = {"chan": partner}
 
     def place(j):
@@ -164,11 +164,14 @@
             )
             for k in range(1, n_s):
                 to, back = lax.rem(s + k, n_s), lax.rem(s + n_s - k, n_s)
-                add(
-                    "relay", None, box.at[mate_frames, own_rows], hop.at[layer, k], {"space": to},
-                    None, hop.at[layer, k], {"space": back},
-                    gr_s.at[layer, k], gr_r.at[layer, k],
-                )
+                for f in range(frames):
+                    add(
+                        "relay" if f == 0 else "relay on",
+                        None, box.at[(q - 1 - r) * frames + f, own_rows], hop.at[layer, k, f],
+                        {"space": to},
+                        None, hop.at[layer, k, f], {"space": back},
+                        gr_s.at[layer, f, k], gr_r.at[layer, f, k],
+                    )
         return found
 
     def when(predicate, action):
@@ -359,7 +362,7 @@
 
     def norm_end(field_ref, base, layer, w_row):
         totals = sums_finish(layer + 1, (r2, r1)[layer])
-        w_ref[w_row : w_row + 1] = totals[1:2]
+        weights[w_row : w_row + 1] = totals[1:2]
         scale = vec[base + 1 : base + 2, mine]
         gain = vec[base + 2 : base + 3, mine]
         means = group_sums(totals * gain, per) / members
@@ -415,7 +418,7 @@
                     for a in range(3):
                         low = a * cs + j * share
                         for c in range(3):
-                            own[a * 9 + b * 3 + c] = product[
+                            own[a, b, c] = product[
                                 low : low + share, c * half : (c + 1) * half
                             ]
 
@@ -455,13 +458,13 @@
             when(go, lambda copy=copy: copy().start())
 
     turn(h_ref, 0)
-    send_fields(fields_two)
     turn(f_ref, 1)
 
     take_moves(moves_two, ("near x",))
     fill_rows(0, r * frames)
     conv(0, k2_ref, True)
     take_moves(moves_two, ("near", "side"))
+    send_fields(fields_two)
     send_moves(moves_two, ("relay",))
     pl.when(t + 1 < n_t)(lambda: fill_rows(0, (r + 1) * frames))
     conv(0, k2_ref, False)
@@ -477,46 +480,64 @@
     vec[6:8] = jnp.zeros((2, channels), F32)
 
     norm_back(h_ref, 3, 0)
+    send_moves(moves_two, ("relay on",))
     send_fields(fields_one)
-    take_fields(fields_two)
-    across(0).start()
-    take_moves(moves_two, ("wide", "relay"))
-    fill_rest(0)
-    across_land(0).wait_recv()
-    activate(0, 3)
     gh[...] = norm_end(h_ref, 3, 0, 1).astype(BF16).reshape(frames, height, padded, half)
     send_moves(moves_one, ("near x", "near"))
     send_moves(moves_one, ("side", "wide"))
     grads[1, own_frames, own_rows] = gh[...]
 
-    delta(0, d2_ref)
-    take_fields(fields_one)
-    across(1).start()
-    across_land(1).wait_recv()
-    activate(1, 0)
-
+    take_fields(fields_two)
+    across(0).start()
+    take_moves(moves_two, ("wide", "relay", "relay on"))
+    fill_rest(0)
+    across_land(0).wait_recv()
+    activate(0, 3)
+    delta(0, d2)
     take_moves(moves_one, ("near x",))
     fill_rows(1, r * frames)
     conv(1, k1_ref, True)
     take_moves(moves_one, ("near", "side"))
-    send_moves(moves_one, ("relay",))
+    send_moves(moves_one, ("relay", "relay on"))
     pl.when(t + 1 < n_t)(lambda: fill_rows(1, (r + 1) * frames))
     conv(1, k1_ref, False)
+    take_fields(fields_one)
+    across(1).start()
     norm_back(f_ref, 0, 1)
-    take_moves(moves_one, ("wide", "relay"))
+    across_land(1).wait_recv()
+    activate(1, 0)
+    take_moves(moves_one, ("wide", "relay", "relay on"))
     fill_rest(1)
-    delta(1, d1_ref)
+    delta(1, d1)
     grad = norm_end(f_ref, 0, 1, 0)
-    fg_ref[...] = (cot_ref[:, :, :, mine].reshape(rows, half).astype(F32) + grad).astype(BF16)
-
-    for layer, own in ((0, d2_ref), (1, d1_ref)):
-        for k in range(1, nj):
-            for b in range(3):
+    total = cot_ref[:, :, :, mine].reshape(rows, half).astype(F32) + grad
+    for f in range(frames):
+        for h in range(height):
+            at = (f * height + h) * padded
+            mixed[f, pl.ds(h, width, stride=height)] = total[at : at + width]
+    fg[...] = mixed[...].astype(BF16)
+    results = [
+        pltpu.make_async_copy(fg, fg_ref, o_sem.at[0]),
+        pltpu.make_async_copy(weights, w_ref, o_sem.at[1]),
+    ]
+    for result in results:
+        result.start()
+
+    for layer, own, target in ((0, d2, d2_ref), (1, d1, d1_ref)):
+        for b in range(3):
+            for k in range(1, nj):
                 block_copy(layer, k, b).wait_recv()
                 for a in range(3):
                     more = got[layer, k, b, a].astype(F32)
                     for c in range(3):
-                        own[a * 9 + b * 3 + c] += more[:, c * half : (c + 1) * half]
+                        own[a, b, c] += more[:, c * half : (c + 1) * half]
+            result = pltpu.make_async_copy(
+                own.at[:, b], target.at[:, b], o_sem.at[2 + 3 * layer + b]
+            )
+            result.start()
+            results.append(result)
+    for result in results:
+        result.wait()
 
     end_moves(moves_two)
     end_moves(moves_one)
@@ -534,6 +555,18 @@
                 block_copy(layer, k, b).wait_send()
 
 
+def hand_over(*refs):
+    sources, targets, sems = refs[:4], refs[4:8], refs[8]
+    copies = [
+        pltpu.make_async_copy(source, target, sems.at[i])
+        for i, (source, target) in enumerate(zip(sources, targets))
+    ]
+    for copy in copies:
+        copy.start()
+    for copy in copies:
+        copy.wait()
+
+
 def shards(n_t, n_s, features, hidden, cotangent, kernel_one, kernel_two, gains):
     frames, height, width, channels = features.shape
     half = kernel_one.shape[4]
@@ -556,20 +589,28 @@
         return kernel.transpose(1, 2, 3, 0, 4).reshape(9, 3, channels, half)
 
     vmem = pl.BlockSpec(memory_space=pltpu.VMEM)
-    hbm = pl.BlockSpec(memory_space=pl.ANY)
+    hbm = pl.BlockSpec(memory_space=pltpu.HBM)
     dma = pltpu.SemaphoreType.DMA
     around = 2 * n_s - 1
-    grad, delta_one, delta_two, weighted = pl.pallas_call(
+    shapes = (
+        jax.ShapeDtypeStruct((frames, height * width, half), BF16),
+        jax.ShapeDtypeStruct((3, 3, 3, share, half), F32),
+        jax.ShapeDtypeStruct((3, 3, 3, share, half), F32),
+        jax.ShapeDtypeStruct((2, half), F32),
+    )
+    passed = pl.BlockSpec(memory_space=pl.ANY)
+    results = pl.pallas_call(
         functools.partial(body, (width, n_t, n_s, q)),
-        out_shape=(
-            jax.ShapeDtypeStruct((rows, half), BF16),
-            jax.ShapeDtypeStruct((27, share, half), F32),
-            jax.ShapeDtypeStruct((27, share, half), F32),
-            jax.ShapeDtypeStruct((2, half), F32),
-        ),
+        out_shape=shapes,
         in_specs=[vmem, vmem, vmem, hbm, hbm, vmem],
-        out_specs=(vmem,) * 4,
+        out_specs=(passed,) * 4,
         scratch_shapes=[
+            pltpu.VMEM((frames, height * width, half), BF16),
+            pltpu.VMEM((frames, height * width, half), F32),
+            pltpu.VMEM((3, 3, 3, share, half), F32),
+            pltpu.VMEM((3, 3, 3, share, half), F32),
+            pltpu.VMEM((2, half), F32),
+            dma((8,)),
             pltpu.VMEM((2, q * frames + 2, tall, padded, half), BF16),
             pltpu.VMEM((2, n_s, frames, height, padded, half), BF16),
             pltpu.VMEM((2, q * frames + 2, tall + 2, padded, 3 * half), BF16),
@@ -592,7 +633,7 @@
             dma((2, 2, around)), dma((2, 2, around)),
             dma((2,)), dma((2,)),
             dma((2, 2)), dma((2, 2)),
-            dma((2, n_s)), dma((2, n_s)),
+            dma((2, frames, n_s)), dma((2, frames, n_s)),
             dma((2,)), dma((2,)),
             dma((2, q, n_s)), dma((2, q, n_s)),
             dma((2, q, n_s)), dma((2, n_s)),
@@ -602,14 +643,23 @@
             dma((3, n)), dma((3, n)),
         ],
         compiler_params=pltpu.CompilerParams(
-            collective_id=0, has_side_effects=True, vmem_limit_bytes=40 * 1024 * 1024
+            collective_id=0, has_side_effects=True, vmem_limit_bytes=51 * 1024 * 1024
         ),
     )(wide(features), wide(hidden), wide(cotangent), stacked(kernel_one), stacked(kernel_two), gains)
 
+    grad, delta_one, delta_two, weighted = pl.pallas_call(
+        hand_over,
+        out_shape=shapes,
+        in_specs=[vmem] * 4,
+        out_specs=(passed,) * 4,
+        scratch_shapes=[dma((4,))],
+        compiler_params=pltpu.CompilerParams(vmem_limit_bytes=8 * 1024 * 1024),
+    )(*results)
+
     def unstacked(delta):
-        return delta.reshape(3, 3, 3, share, half).transpose(3, 0, 1, 2, 4)
-
-    feature_grad = grad.reshape(frames, height, padded, half)[:, :, :width]
+        return delta.transpose(3, 0, 1, 2, 4)
+
+    feature_grad = grad.reshape(frames, width, height, half).transpose(0, 2, 1, 3)
     return (feature_grad, unstacked(delta_one), unstacked(delta_two), weighted)
 
 

time: 57.4 us -> 52.5 us (0.915)
  local copies, waits for them, and re-layouts: 5.91 us -> 1.75 us
  Pallas kernels: 50.6 us -> 49.9 us
    unnamed x17 -> x9, local copies, waits for them, and re-layouts: 5.81 us -> 1.65 us
    pallas_call x1 -> x2, Pallas kernels: 50.6 us -> 49.9 us  [the longest x1 48.9 us: shards(): pl.pallas_call(functools.partial(body, (width, n_t, n_s, q)), out_shape=s...]
where the time goes in v3:
time: 52.5 us; the launch traced here: 52.4 us
  Pallas kernels  49.9 us (95%)
  local copies, waits for them, and re-layouts  1.75 us (3%)
  between operations  0.72 us (1%)
    pallas_call x1, Pallas kernels, shards(): pl.pallas_call(functools.partial(body, (width, n_t, n_s, q)), out_shape=s...  48.9 us
    unnamed x9, local copies, waits for them, and re-layouts  1.65 us

profile of v3, /device:TPU:0, one launch (start us, length us, event | category | flops | bytes accessed | tf_op | source)
XLA Modules:
  0.0 52.4 jit_solution(7038298908897869157)
XLA Ops:
  0.6 0.0 copy-start.2
  0.6 0.0 copy-start.1
  0.7 1.1 %copy.10 = bf16[2,4,90,256]{3,2,1,0:T(8,128)(2,1)S(1)} copy(bf16[2,4,90,256]{3,1,2,0:T(4,128)(2,1)} %param.6) | data formatting | bytes 737280 | tf_op args[0]
  1.8 0.0 copy-start
  1.8 0.0 copy-done.1
  1.9 0.0 copy-done.2
  2.0 0.4 copy-done
  2.5 48.9 %shard_map.93 = (bf16[2,360,128]{2,1,0:T(8,128)(2,1)S(1)}, f32[3,3,3,32,128]{4,3,2,1,0:T(8,128)S(1)}, f32[3,3,3,32,128]{4,3,2,1,0:T(8,128)S(1)}, f32[2,128]{1,0:T(2,128)S(1)}) custom-call(bf16[2,4,96,256]{3,2,1,0:T(8,128)(2,1)S(1)} %pad.10.f_ref, bf16[2,4,96,256]{3,2,1,0:T(8,128)(2,1)S(1)} %pad.11.h_ref, bf16[2,4,96,256]{3,2,1,0:T(8,128)(2,1)S(1)} %pad.12.cot_ref, ...), custom_call_target="tpu_custom_call" | custom-call | tf_op jit(solution)/shard_map/pallas_call | solution.py:602
  51.4 1.0 %shard_map.94 = (bf16[2,360,128]{2,1,0:T(8,128)(2,1)}, f32[3,3,3,32,128]{4,3,2,1,0:T(8,128)}, f32[3,3,3,32,128]{4,3,2,1,0:T(8,128)}, f32[2,128]{1,0:T(2,128)}) custom-call(bf16[2,360,128]{2,1,0:T(8,128)(2,1)S(1)} %get-tuple-element.12.refs_0_, f32[3,3,3,32,128]{4,3,2,1,0:T(8,128)S(1)} %get-tuple-element.13.refs_1_, ...), custom_call_target="tpu_custom_call" | custom-call | tf_op jit(solution)/shard_map/pallas_call | solution.py:650
  (5 shorter events, 0.2 us)
Async XLA Ops:
  0.6 1.3 %copy-start.2 = (bf16[2,4,90,256]{3,1,2,0:T(4,128)(2,1)S(1)}, bf16[2,4,90,256]{3,1,2,0:T(4,128)(2,1)}, u32[]{:S(2)}) copy-start(bf16[2,4,90,256]{3,1,2,0:T(4,128)(2,1)} %param.8) | copy-start | bytes 1105924
  0.6 1.2 %copy-start.1 = (bf16[2,4,90,256]{3,1,2,0:T(4,128)(2,1)S(1)}, bf16[2,4,90,256]{3,1,2,0:T(4,128)(2,1)}, u32[]{:S(2)}) copy-start(bf16[2,4,90,256]{3,1,2,0:T(4,128)(2,1)} %param.7) | copy-start | bytes 1105924
  1.8 0.7 %copy-start = (f32[2,256]{1,0:T(2,128)S(1)}, f32[2,256]{1,0:T(2,128)}, u32[]{:S(2)}) copy-start(f32[2,256]{1,0:T(2,128)} %gain_ref.1) | copy-start | bytes 6148

commit v4 on v3

--- a/solution.py
+++ b/solution.py
@@ -24,9 +24,9 @@
 
 def body(
     sizes,
-    f_ref, h_ref, cot_ref, k1_ref, k2_ref, gain_ref,
+    f_ref, h_ref, cot_ref, k1_ref, k2_ref, gain_hbm,
     fg_ref, d1_ref, d2_ref, w_ref,
-    fg, mixed, d1, d2, weights, o_sem,
+    fg, mixed, d1, d2, weights, gain_ref, o_sem,
     grads, hop, taps, gh, kcat, turned, raw, act, acc, xs, xr, vec, r0, r2, r1, out, got, perm,
     k_sem, gx_s, gx_r, gz_s, gz_r, ge_s, ge_r, gr_s, gr_r, gg_s, gg_r,
     ai_s, ai_r, an_s, an_r, ad_s, ad_r, dl_s, dl_r, xsem_s, xsem_r, ar_s, ar_r,
@@ -79,13 +79,16 @@
 
     def kernel_copy(layer, source, c):
         return pltpu.make_async_copy(
-            source.at[:, c], kcat.at[layer, :, :, c * half : (c + 1) * half], k_sem.at[layer, c]
+            source.at[:, c], kcat.at[layer, :, :, c * half : (c + 1) * half], k_sem.at[layer]
         )
 
     for c in range(3):
         kernel_copy(0, k2_ref, c).start()
     for c in range(3):
         kernel_copy(1, k1_ref, c).start()
+
+    gain_copy = pltpu.make_async_copy(gain_hbm, gain_ref, o_sem.at[4])
+    gain_copy.start()
 
     barrier = pltpu.get_barrier_semaphore()
     pl.semaphore_signal(barrier, inc=1, device_id=sibling, device_id_type=MESH)
@@ -116,16 +119,17 @@
         before = jnp.where(r > 0, r, q) * frames
         sent = pl.ds(before, frames)
 
-        def add(kind, go, src, dst, to, come, land, sender, send, recv):
+        def add(kind, go, src, dst, to, come, land, sender, send, recv, ends):
             found.append((
                 kind, go, lambda: remote(src, dst, send, recv, to),
-                come, lambda: remote(land, land, send, recv, sender),
+                come, None if land is None else lambda: remote(land, land, send, recv, sender),
+                None if ends is None else lambda: remote(ends, ends, send, recv, to),
             ))
 
         for d, (ds, row) in enumerate(((1, height - 1), (-1, 0))):
             back = (s - ds) * height + row
             add(
-                "near",
+                "near edge",
                 (t > 0) & inside(s + ds, n_s),
                 source.at[:, row : row + 1],
                 box.at[sent, pl.ds(s * height + row, 1)],
@@ -133,15 +137,16 @@
                 (t + 1 < n_t) & inside(s - ds, n_s),
                 box.at[next_frames, pl.ds(back, 1)],
                 {"tm": t + 1, "space": s - ds},
-                ge_s.at[layer, d], ge_r.at[layer, d],
+                ge_s.at[layer, d], ge_r.at[layer, d], source.at[:, row : row + 1],
             )
-        add(
-            "near", t > 0, source, box.at[sent, own_rows], {"tm": t - 1},
-            t + 1 < n_t, box.at[next_frames, own_rows], {"tm": t + 1},
-            gz_s.at[layer], gz_r.at[layer],
-        )
+        for f in range(frames):
+            add(
+                f"near {f}", t > 0, source.at[f], box.at[before + f, own_rows], {"tm": t - 1},
+                t + 1 < n_t, box.at[(r + 1) * frames + f, own_rows], {"tm": t + 1},
+                gz_s.at[layer], gz_r.at[layer, f], source if f == 0 else None,
+            )
         for k in sorted((k for k in range(1 - n_s, n_s) if k), key=abs):
-            i = k + n_s - 1
+            i = k + n_s - 1 if k < 0 else k + n_s - 2
             spans = (("wide", 0, height),)
             if abs(k) == 1:
                 spans = (("near x", height - 1, 1), ("wide", 0, height - 1))
@@ -153,24 +158,26 @@
                     box.at[own_frames, pl.ds(s * height + low, count)], {"space": s + k},
                     inside(s - k, n_s),
                     box.at[own_frames, pl.ds((s - k) * height + low, count)], {"space": s - k},
-                    gx_s.at[layer, part, i], gx_r.at[layer, part, i],
+                    gx_s.at[layer, i], gx_r.at[layer, part, i], source if part == 0 else None,
                 )
         if q > 1:
-            earlier = pl.ds((r - 1) * frames, frames)
-            add(
-                "side", r < q - 1, source, box.at[own_frames, own_rows], {"tm": t + 1},
-                r > 0, box.at[earlier, own_rows], {"tm": t - 1},
-                gg_s.at[layer], gg_r.at[layer],
-            )
+            for f in range(frames):
+                add(
+                    f"side {f}", r < q - 1,
+                    source.at[f], box.at[r * frames + f, own_rows], {"tm": t + 1},
+                    r > 0, box.at[(r - 1) * frames + f, own_rows], {"tm": t - 1},
+                    gg_s.at[layer], gg_r.at[layer, f], source if f == 0 else None,
+                )
             for k in range(1, n_s):
                 to, back = lax.rem(s + k, n_s), lax.rem(s + n_s - k, n_s)
                 for f in range(frames):
                     add(
-                        "relay" if f == 0 else "relay on",
+                        f"relay {f}",
                         None, box.at[(q - 1 - r) * frames + f, own_rows], hop.at[layer, k, f],
                         {"space": to},
-                        None, hop.at[layer, k, f], {"space": back},
-                        gr_s.at[layer, f, k], gr_r.at[layer, f, k],
+                        None, hop.at[layer, k] if f == 0 else None, {"space": back},
+                        gr_s.at[layer, k - 1], gr_r.at[layer, k - 1],
+                        hop.at[layer, k] if f == 0 else None,
                     )
         return found
 
@@ -181,18 +188,19 @@
             pl.when(predicate)(action)
 
     def send_moves(found, kinds):
-        for kind, go, copy, _, _ in found:
-            if kind in kinds:
+        for kind, go, copy, *_ in found:
+            if kind.startswith(kinds):
                 when(go, lambda copy=copy: copy().start())
 
     def take_moves(found, kinds):
-        for kind, _, _, come, copy in found:
-            if kind in kinds:
+        for kind, _, _, come, copy, _ in found:
+            if kind.startswith(kinds) and copy is not None:
                 when(come, lambda copy=copy: copy().wait_recv())
 
     def end_moves(found):
-        for _, go, copy, _, _ in found:
-            when(go, lambda copy=copy: copy().wait_send())
+        for _, go, _, _, _, copy in found:
+            if copy is not None:
+                when(go, lambda copy=copy: copy().wait_send())
 
     def set_rows(to_r, to_s):
         start = (to_r * n_s + to_s) * cs + chan * hc
@@ -210,36 +218,46 @@
                 if dr == 0 and k == 0:
                     continue
                 to_r, to_s = lax.rem(r + dr, q), lax.rem(s + k, n_s)
-                from_r, from_s = lax.rem(r + q - dr, q), lax.rem(s + n_s - k, n_s)
                 src = turned.at[layer, :, set_rows(to_r, to_s)]
                 dst = raw.at[layer, pl.ds(2 + r * frames, frames), my_half, strip(s)]
-                land = raw.at[layer, pl.ds(2 + from_r * frames, frames), my_half, strip(from_s)]
-                sems = (ai_s.at[layer, dr, k], ai_r.at[layer, dr, k])
-                found.append((
-                    "in", None,
-                    functools.partial(remote, src, dst, *sems, {"tm": p * q + to_r, "space": to_s}),
-                    None,
-                    functools.partial(remote, land, land, *sems, {"tm": p * q + from_r, "space": from_s}),
-                ))
+                found.append((None, functools.partial(
+                    remote, src, dst, ai_s.at[layer], ai_r.at[layer],
+                    {"tm": p * q + to_r, "space": to_s},
+                )))
         for to_r in range(q):
             for k in range(n_s):
-                to_s, from_s = lax.rem(s + k, n_s), lax.rem(s + n_s - k, n_s)
+                to_s = lax.rem(s + k, n_s)
                 src = turned.at[layer, frames - 2 : frames, set_rows(to_r, to_s)]
                 dst = raw.at[layer, 0:2, my_half, strip(s)]
-                land = raw.at[layer, 0:2, my_half, strip(from_s)]
-                sems = (an_s.at[layer, to_r, k], an_r.at[layer, k])
-                found.append((
-                    "on", (r == q - 1) & (p + 1 < nj),
-                    functools.partial(remote, src, dst, *sems, {"tm": (p + 1) * q + to_r, "space": to_s}),
-                    (p > 0) if to_r == 0 else False,
-                    functools.partial(remote, land, land, *sems, {"tm": p * q - 1, "space": from_s}),
-                ))
+                found.append(((r == q - 1) & (p + 1 < nj), functools.partial(
+                    remote, src, dst, an_s.at[layer], an_r.at[layer],
+                    {"tm": (p + 1) * q + to_r, "space": to_s},
+                )))
         return found
 
-    def take_fields(found):
-        for _, _, _, come, copy in found:
-            if come is not False:
-                when(come, lambda copy=copy: copy().wait_recv())
+    def send_fields(found):
+        for go, copy in found:
+            when(go, lambda copy=copy: copy().start())
+
+    def fields_like(layer, count, first, send, recv):
+        cells = turned.at[layer, first:frames, 0 : count * hc]
+        return remote(cells, cells, send.at[layer], recv.at[layer], sibling)
+
+    def take_fields(layer):
+        if q * n_s > 1:
+            fields_like(layer, q * n_s - 1, 0, ai_s, ai_r).wait_recv()
+
+        @pl.when(p > 0)
+        def _():
+            fields_like(layer, n_s, frames - 2, an_s, an_r).wait_recv()
+
+    def end_fields(layer):
+        if q * n_s > 1:
+            fields_like(layer, q * n_s - 1, 0, ai_s, ai_r).wait_send()
+
+        @pl.when((r == q - 1) & (p + 1 < nj))
+        def _():
+            fields_like(layer, q * n_s, frames - 2, an_s, an_r).wait_send()
 
     def across(layer):
         half_set = raw.at[layer, :, my_half]
@@ -249,26 +267,24 @@
         other = raw.at[layer, :, pl.ds(pl.multiple_of(partner * hc, hc), hc)]
         return remote(other, other, ad_s.at[layer], ad_r.at[layer], sibling)
 
-    def sums_copy(layer, buf, k, slot):
-        return remote(
-            buf.at[slot], buf.at[slot], ar_s.at[layer, k], ar_r.at[layer, slot], place(peer(k))
-        )
+    def sums_copy(layer, buf, device, part):
+        return remote(part, part, ar_s.at[layer], ar_r.at[layer], device)
 
     def sums_start(layer, buf, values):
         buf[rank] = values
-        each_peer(lambda k: sums_copy(layer, buf, k, rank).start())
+        each_peer(lambda k: sums_copy(layer, buf, place(peer(k)), buf.at[rank]).start())
 
     def sums_finish(layer, buf):
-        each_peer(lambda k: sums_copy(layer, buf, k, peer(k)).wait_recv())
+        sums_copy(layer, buf, sibling, buf.at[0 : n - 1]).wait_recv()
         return jnp.sum(buf[...], axis=0)
 
     def sums_end(layer, buf):
-        each_peer(lambda k: sums_copy(layer, buf, k, rank).wait_send())
+        sums_copy(layer, buf, sibling, buf.at[0 : n - 1]).wait_send()
 
     def block_copy(layer, k, b):
         to = lax.rem(p + k, nj)
         return remote(
-            out.at[layer, to, b], got.at[layer, k, b], dl_s.at[layer, k, b], dl_r.at[layer, k, b],
+            out.at[layer, to, b], got.at[layer, k, b], dl_s.at[layer, k - 1], dl_r.at[layer, k - 1, b],
             {"tm": to * q + r},
         )
 
@@ -292,14 +308,23 @@
     def fill(layer, f, row, count):
         spread(layer, f, row, grads[layer, f, pl.ds(row, count)])
 
-    def fill_rows(layer, first):
+    def fill_rows(layer, f):
+        fill(layer, f, s * height, height)
+        for row, ok in ((s * height - 1, s > 0), ((s + 1) * height, s + 1 < n_s)):
+            pl.when(ok)(functools.partial(fill, layer, f, row, 1))
+
+    def land(layer):
+        take_moves(moves_of[layer], ("near edge",))
         for f in range(frames):
-            fill(layer, first + f, s * height, height)
-        for row, ok in ((s * height - 1, s > 0), ((s + 1) * height, s + 1 < n_s)):
-            @pl.when(ok)
-            def _(row=row):
-                for f in range(frames):
-                    fill(layer, first + f, row, 1)
+            take_moves(moves_of[layer], (f"near {f}", f"side {f}"))
+            if layer == 1 or f == 0:
+                send_moves(moves_of[layer], (f"relay {f}",))
+            pl.when(t + 1 < n_t)(functools.partial(fill_rows, layer, (r + 1) * frames + f))
+
+    def fill_own(layer):
+        take_moves(moves_of[layer], ("near x",))
+        for f in range(frames):
+            fill_rows(layer, r * frames + f)
 
     def fill_rest(layer):
         for k in range(1, n_s):
@@ -317,8 +342,7 @@
 
     def conv(layer, source, near):
         if near:
-            for c in range(3):
-                kernel_copy(layer, source, c).wait()
+            pltpu.make_async_copy(kcat.at[layer], kcat.at[layer], k_sem.at[layer]).wait()
         for f in range(frames):
             total = None
             for ab in range(9):
@@ -425,10 +449,9 @@
             for k in range(1, nj):
                 block_copy(layer, k, b).start()
 
-    moves_two = moves(0, cot_ref.at[:, :, :, mine])
-    moves_one = moves(1, gh)
-    send_moves(moves_two, ("near x", "near"))
-    send_moves(moves_two, ("side", "wide"))
+    moves_of = (moves(0, cot_ref.at[:, :, :, mine]), moves(1, gh))
+    send_moves(moves_of[0], ("near", "side"))
+    send_moves(moves_of[0], ("wide",))
     grads[0, own_frames, own_rows] = cot_ref[:, :, :, mine]
 
     field_one = f_ref[...].reshape(rows, channels).astype(F32)
@@ -453,21 +476,15 @@
     fields_two = field_moves(0)
     fields_one = field_moves(1)
 
-    def send_fields(found):
-        for _, go, copy, _, _ in found:
-            when(go, lambda copy=copy: copy().start())
-
     turn(h_ref, 0)
     turn(f_ref, 1)
 
-    take_moves(moves_two, ("near x",))
-    fill_rows(0, r * frames)
+    fill_own(0)
     conv(0, k2_ref, True)
-    take_moves(moves_two, ("near", "side"))
+    land(0)
     send_fields(fields_two)
-    send_moves(moves_two, ("relay",))
-    pl.when(t + 1 < n_t)(lambda: fill_rows(0, (r + 1) * frames))
     conv(0, k2_ref, False)
+    gain_copy.wait()
 
     totals = group_sums(sums_finish(0, r0), per) / members
     mean_one, mean_two = totals[0:1], totals[2:3]
@@ -480,33 +497,31 @@
     vec[6:8] = jnp.zeros((2, channels), F32)
 
     norm_back(h_ref, 3, 0)
-    send_moves(moves_two, ("relay on",))
+    for f in range(1, frames):
+        send_moves(moves_of[0], (f"relay {f}",))
     send_fields(fields_one)
     gh[...] = norm_end(h_ref, 3, 0, 1).astype(BF16).reshape(frames, height, padded, half)
-    send_moves(moves_one, ("near x", "near"))
-    send_moves(moves_one, ("side", "wide"))
+    send_moves(moves_of[1], ("near", "side"))
+    send_moves(moves_of[1], ("wide",))
     grads[1, own_frames, own_rows] = gh[...]
 
-    take_fields(fields_two)
+    take_fields(0)
     across(0).start()
-    take_moves(moves_two, ("wide", "relay", "relay on"))
+    take_moves(moves_of[0], ("wide", "relay"))
     fill_rest(0)
     across_land(0).wait_recv()
     activate(0, 3)
     delta(0, d2)
-    take_moves(moves_one, ("near x",))
-    fill_rows(1, r * frames)
+    fill_own(1)
     conv(1, k1_ref, True)
-    take_moves(moves_one, ("near", "side"))
-    send_moves(moves_one, ("relay", "relay on"))
-    pl.when(t + 1 < n_t)(lambda: fill_rows(1, (r + 1) * frames))
+    land(1)
     conv(1, k1_ref, False)
-    take_fields(fields_one)
+    take_fields(1)
     across(1).start()
     norm_back(f_ref, 0, 1)
     across_land(1).wait_recv()
     activate(1, 0)
-    take_moves(moves_one, ("wide", "relay", "relay on"))
+    take_moves(moves_of[1], ("wide", "relay"))
     fill_rest(1)
     delta(1, d1)
     grad = norm_end(f_ref, 0, 1, 0)
@@ -532,18 +547,17 @@
                     for c in range(3):
                         own[a, b, c] += more[:, c * half : (c + 1) * half]
             result = pltpu.make_async_copy(
-                own.at[:, b], target.at[:, b], o_sem.at[2 + 3 * layer + b]
+                own.at[:, b], target.at[:, b], o_sem.at[2 + layer]
             )
             result.start()
-            results.append(result)
+        results.append(pltpu.make_async_copy(own, target, o_sem.at[2 + layer]))
     for result in results:
         result.wait()
 
-    end_moves(moves_two)
-    end_moves(moves_one)
-    for found in (fields_two, fields_one):
-        for _, go, copy, _, _ in found:
-            when(go, lambda copy=copy: copy().wait_send())
+    end_moves(moves_of[0])
+    end_moves(moves_of[1])
+    end_fields(0)
+    end_fields(1)
     sums_end(0, r0)
     sums_end(1, r2)
     sums_end(2, r1)
@@ -551,8 +565,8 @@
         cross(layer).wait_send()
         across(layer).wait_send()
         for k in range(1, nj):
-            for b in range(3):
-                block_copy(layer, k, b).wait_send()
+            whole = out.at[layer, 0]
+            remote(whole, whole, dl_s.at[layer, k - 1], dl_r.at[layer, k - 1, 0], sibling).wait_send()
 
 
 def hand_over(*refs):
@@ -591,7 +605,6 @@
     vmem = pl.BlockSpec(memory_space=pltpu.VMEM)
     hbm = pl.BlockSpec(memory_space=pltpu.HBM)
     dma = pltpu.SemaphoreType.DMA
-    around = 2 * n_s - 1
     shapes = (
         jax.ShapeDtypeStruct((frames, height * width, half), BF16),
         jax.ShapeDtypeStruct((3, 3, 3, share, half), F32),
@@ -602,7 +615,7 @@
     results = pl.pallas_call(
         functools.partial(body, (width, n_t, n_s, q)),
         out_shape=shapes,
-        in_specs=[vmem, vmem, vmem, hbm, hbm, vmem],
+        in_specs=[vmem, vmem, vmem, hbm, hbm, hbm],
         out_specs=(passed,) * 4,
         scratch_shapes=[
             pltpu.VMEM((frames, height * width, half), BF16),
@@ -610,7 +623,8 @@
             pltpu.VMEM((3, 3, 3, share, half), F32),
             pltpu.VMEM((3, 3, 3, share, half), F32),
             pltpu.VMEM((2, half), F32),
-            dma((8,)),
+            pltpu.VMEM((2, channels), F32),
+            dma((5,)),
             pltpu.VMEM((2, q * frames + 2, tall, padded, half), BF16),
             pltpu.VMEM((2, n_s, frames, height, padded, half), BF16),
             pltpu.VMEM((2, q * frames + 2, tall + 2, padded, 3 * half), BF16),
@@ -629,18 +643,18 @@
             pltpu.VMEM((2, nj, 3, 3, share, 3 * half), BF16),
             pltpu.VMEM((2, nj, 3, 3, share, 3 * half), BF16),
             pltpu.VMEM((channels, channels), BF16),
-            dma((2, 3)),
-            dma((2, 2, around)), dma((2, 2, around)),
+            dma((2,)),
+            dma((2, 2 * n_s - 2)), dma((2, 2, 2 * n_s - 2)),
+            dma((2,)), dma((2, frames)),
+            dma((2, 2)), dma((2, 2)),
+            dma((2, n_s - 1)), dma((2, n_s - 1)),
+            dma((2,)), dma((2, frames)),
             dma((2,)), dma((2,)),
-            dma((2, 2)), dma((2, 2)),
-            dma((2, frames, n_s)), dma((2, frames, n_s)),
             dma((2,)), dma((2,)),
-            dma((2, q, n_s)), dma((2, q, n_s)),
-            dma((2, q, n_s)), dma((2, n_s)),
             dma((2,)), dma((2,)),
-            dma((2, nj, 3)), dma((2, nj, 3)),
+            dma((2, nj - 1)), dma((2, nj - 1, 3)),
             dma((2,)), dma((2,)),
-            dma((3, n)), dma((3, n)),
+            dma((3,)), dma((3,)),
         ],
         compiler_params=pltpu.CompilerParams(
             collective_id=0, has_side_effects=True, vmem_limit_bytes=51 * 1024 * 1024

time: 52.5 us -> 50.9 us (0.970)
  Pallas kernels: 49.9 us -> 48.3 us
    pallas_call x1, Pallas kernels: 48.9 us -> 47.3 us  [shards(): pl.pallas_call(functools.partial(body, (width, n_t, n_s, q)), out_shape=s...]
where the time goes in v4:
time: 50.9 us; the launch traced here: 50.7 us
  Pallas kernels  48.3 us (95%)
  local copies, waits for them, and re-layouts  1.75 us (3%)
  between operations  0.72 us (1%)
    pallas_call x1, Pallas kernels, shards(): pl.pallas_call(functools.partial(body, (width, n_t, n_s, q)), out_shape=s...  47.3 us
    unnamed x9, local copies, waits for them, and re-layouts  1.65 us

profile of v4, /device:TPU:0, one launch (start us, length us, event | category | flops | bytes accessed | tf_op | source)
XLA Modules:
  0.0 50.7 jit_solution(10208807506856577711)
XLA Ops:
  0.6 0.0 copy-start.2
  0.6 0.0 copy-start.1
  0.7 1.1 %copy.10 = bf16[2,4,90,256]{3,2,1,0:T(8,128)(2,1)S(1)} copy(bf16[2,4,90,256]{3,1,2,0:T(4,128)(2,1)} %param.6) | data formatting | bytes 737280 | tf_op args[0]
  1.8 0.0 copy-start
  1.8 0.0 copy-done.1
  1.9 0.0 copy-done.2
  2.0 0.4 copy-done
  2.5 47.3 %shard_map.93 = (bf16[2,360,128]{2,1,0:T(8,128)(2,1)S(1)}, f32[3,3,3,32,128]{4,3,2,1,0:T(8,128)S(1)}, f32[3,3,3,32,128]{4,3,2,1,0:T(8,128)S(1)}, f32[2,128]{1,0:T(2,128)S(1)}) custom-call(bf16[2,4,96,256]{3,2,1,0:T(8,128)(2,1)S(1)} %pad.10.f_ref, bf16[2,4,96,256]{3,2,1,0:T(8,128)(2,1)S(1)} %pad.11.h_ref, bf16[2,4,96,256]{3,2,1,0:T(8,128)(2,1)S(1)} %pad.12.cot_ref, ...), custom_call_target="tpu_custom_call" | custom-call | tf_op jit(solution)/shard_map/pallas_call | solution.py:615
  49.7 1.0 %shard_map.94 = (bf16[2,360,128]{2,1,0:T(8,128)(2,1)}, f32[3,3,3,32,128]{4,3,2,1,0:T(8,128)}, f32[3,3,3,32,128]{4,3,2,1,0:T(8,128)}, f32[2,128]{1,0:T(2,128)}) custom-call(bf16[2,360,128]{2,1,0:T(8,128)(2,1)S(1)} %get-tuple-element.12.refs_0_, f32[3,3,3,32,128]{4,3,2,1,0:T(8,128)S(1)} %get-tuple-element.13.refs_1_, ...), custom_call_target="tpu_custom_call" | custom-call | tf_op jit(solution)/shard_map/pallas_call | solution.py:664
  (5 shorter events, 0.2 us)
Async XLA Ops:
  0.6 1.3 %copy-start.2 = (bf16[2,4,90,256]{3,1,2,0:T(4,128)(2,1)S(1)}, bf16[2,4,90,256]{3,1,2,0:T(4,128)(2,1)}, u32[]{:S(2)}) copy-start(bf16[2,4,90,256]{3,1,2,0:T(4,128)(2,1)} %param.8) | copy-start | bytes 1105924
  0.6 1.2 %copy-start.1 = (bf16[2,4,90,256]{3,1,2,0:T(4,128)(2,1)S(1)}, bf16[2,4,90,256]{3,1,2,0:T(4,128)(2,1)}, u32[]{:S(2)}) copy-start(bf16[2,4,90,256]{3,1,2,0:T(4,128)(2,1)} %param.7) | copy-start | bytes 1105924
  1.8 0.7 %copy-start = (f32[2,256]{1,0:T(2,128)S(1)}, f32[2,256]{1,0:T(2,128)}, u32[]{:S(2)}) copy-start(f32[2,256]{1,0:T(2,128)} %gain_hbm.1) | copy-start | bytes 6148

commit v5 on v4

--- a/solution.py
+++ b/solution.py
@@ -8,6 +8,7 @@
 from jax.sharding import PartitionSpec as P
 
 GROUPS = 32
+SOON = 2
 EPS = 1e-06
 MESH = pl.DeviceIdType.MESH
 F32 = jnp.float32
@@ -50,6 +51,7 @@
     rank = t * n_s + s
     r = lax.rem(t, q)
     p = t // q
+    held = (r == q - 1) & (p > 0)
     members = float(frames * height * width * per * n)
     mine = pl.ds(pl.multiple_of(chan * half, half), half)
     theirs = pl.ds(pl.multiple_of(partner * half, half), half)
@@ -447,7 +449,8 @@
                             ]
 
             for k in range(1, nj):
-                block_copy(layer, k, b).start()
+                now = ~held | (p + k < nj) if layer == 1 and b >= SOON else None
+                when(now, lambda k=k, b=b: block_copy(layer, k, b).start())
 
     moves_of = (moves(0, cot_ref.at[:, :, :, mine]), moves(1, gh))
     send_moves(moves_of[0], ("near", "side"))
@@ -538,10 +541,19 @@
     for result in results:
         result.start()
 
+    if nj > 1:
+        @pl.when(held)
+        def _():
+            block_copy(1, 1, 0).wait_recv()
+            for k in range(1, nj):
+                for b in range(SOON, 3):
+                    pl.when(p + k >= nj)(lambda k=k, b=b: block_copy(1, k, b).start())
+
     for layer, own, target in ((0, d2, d2_ref), (1, d1, d1_ref)):
         for b in range(3):
             for k in range(1, nj):
-                block_copy(layer, k, b).wait_recv()
+                early = layer == 1 and k == 1 and b == 0
+                when(~held if early else None, lambda k=k, b=b: block_copy(layer, k, b).wait_recv())
                 for a in range(3):
                     more = got[layer, k, b, a].astype(F32)
                     for c in range(3):

time: 50.9 us -> 49.3 us (0.969)
  Pallas kernels: 48.3 us -> 46.7 us
    pallas_call x1, Pallas kernels: 47.3 us -> 45.7 us  [shards(): pl.pallas_call(functools.partial(body, (width, n_t, n_s, q)), out_shape=s...]
where the time goes in v5:
time: 49.3 us; the launch traced here: 49.2 us
  Pallas kernels  46.7 us (95%)
  local copies, waits for them, and re-layouts  1.75 us (4%)
  between operations  0.72 us (1%)
    pallas_call x1, Pallas kernels, shards(): pl.pallas_call(functools.partial(body, (width, n_t, n_s, q)), out_shape=s...  45.7 us
    unnamed x9, local copies, waits for them, and re-layouts  1.65 us
    pallas_call x1, Pallas kernels, shards(): pl.pallas_call(hand_over, out_shape=shapes, in_specs=[vmem] * 4, out_spec...  1.01 us

profile of v5, /device:TPU:0, one launch (start us, length us, event | category | flops | bytes accessed | tf_op | source)
XLA Modules:
  0.0 49.2 jit_solution(14400098955755832515)
XLA Ops:
  0.6 0.0 copy-start.2
  0.6 0.0 copy-start.1
  0.7 1.1 %copy.10 = bf16[2,4,90,256]{3,2,1,0:T(8,128)(2,1)S(1)} copy(bf16[2,4,90,256]{3,1,2,0:T(4,128)(2,1)} %param.6) | data formatting | bytes 737280 | tf_op args[0]
  1.8 0.0 copy-start
  1.8 0.0 copy-done.1
  1.9 0.0 copy-done.2
  2.0 0.4 copy-done
  2.5 45.7 %shard_map.93 = (bf16[2,360,128]{2,1,0:T(8,128)(2,1)S(1)}, f32[3,3,3,32,128]{4,3,2,1,0:T(8,128)S(1)}, f32[3,3,3,32,128]{4,3,2,1,0:T(8,128)S(1)}, f32[2,128]{1,0:T(2,128)S(1)}) custom-call(bf16[2,4,96,256]{3,2,1,0:T(8,128)(2,1)S(1)} %pad.10.f_ref, bf16[2,4,96,256]{3,2,1,0:T(8,128)(2,1)S(1)} %pad.11.h_ref, bf16[2,4,96,256]{3,2,1,0:T(8,128)(2,1)S(1)} %pad.12.cot_ref, ...), custom_call_target="tpu_custom_call" | custom-call | tf_op jit(solution)/shard_map/pallas_call | solution.py:627
  48.2 1.0 %shard_map.94 = (bf16[2,360,128]{2,1,0:T(8,128)(2,1)}, f32[3,3,3,32,128]{4,3,2,1,0:T(8,128)}, f32[3,3,3,32,128]{4,3,2,1,0:T(8,128)}, f32[2,128]{1,0:T(2,128)}) custom-call(bf16[2,360,128]{2,1,0:T(8,128)(2,1)S(1)} %get-tuple-element.12.refs_0_, f32[3,3,3,32,128]{4,3,2,1,0:T(8,128)S(1)} %get-tuple-element.13.refs_1_, ...), custom_call_target="tpu_custom_call" | custom-call | tf_op jit(solution)/shard_map/pallas_call | solution.py:676
  (5 shorter events, 0.2 us)
Async XLA Ops:
  0.6 1.3 %copy-start.2 = (bf16[2,4,90,256]{3,1,2,0:T(4,128)(2,1)S(1)}, bf16[2,4,90,256]{3,1,2,0:T(4,128)(2,1)}, u32[]{:S(2)}) copy-start(bf16[2,4,90,256]{3,1,2,0:T(4,128)(2,1)} %param.8) | copy-start | bytes 1105924
  0.6 1.2 %copy-start.1 = (bf16[2,4,90,256]{3,1,2,0:T(4,128)(2,1)S(1)}, bf16[2,4,90,256]{3,1,2,0:T(4,128)(2,1)}, u32[]{:S(2)}) copy-start(bf16[2,4,90,256]{3,1,2,0:T(4,128)(2,1)} %param.7) | copy-start | bytes 1105924
  1.8 0.7 %copy-start = (f32[2,256]{1,0:T(2,128)S(1)}, f32[2,256]{1,0:T(2,128)}, u32[]{:S(2)}) copy-start(f32[2,256]{1,0:T(2,128)} %gain_hbm.1) | copy-start | bytes 6148

commit v6 on v5

--- a/solution.py
+++ b/solution.py
@@ -8,7 +8,6 @@
 from jax.sharding import PartitionSpec as P
 
 GROUPS = 32
-SOON = 2
 EPS = 1e-06
 MESH = pl.DeviceIdType.MESH
 F32 = jnp.float32
@@ -97,19 +96,6 @@
     each_peer(
         lambda k: pl.semaphore_signal(barrier, inc=1, device_id=place(peer(k)), device_id_type=MESH)
     )
-    for layer in range(2):
-        edge = jnp.zeros((q * frames + 2, 1, padded, 3 * half), BF16)
-        taps[layer, :, 0:1] = edge
-        taps[layer, :, tall + 1 : tall + 2] = edge
-
-        @pl.when(t == n_t - 1)
-        def _(layer=layer):
-            def clear(f, carry):
-                taps[layer, q * frames + f] = jnp.zeros((tall + 2, padded, 3 * half), BF16)
-                return carry
-
-            lax.fori_loop(0, 2, clear, 0)
-
     pl.semaphore_wait(barrier, n)
 
     def inside(value, count):
@@ -449,12 +435,25 @@
                             ]
 
             for k in range(1, nj):
-                now = ~held | (p + k < nj) if layer == 1 and b >= SOON else None
+                now = ~held | (p + k < nj) | (b < 2 - chan) if layer == 1 and b > 0 else None
                 when(now, lambda k=k, b=b: block_copy(layer, k, b).start())
 
     moves_of = (moves(0, cot_ref.at[:, :, :, mine]), moves(1, gh))
     send_moves(moves_of[0], ("near", "side"))
     send_moves(moves_of[0], ("wide",))
+    for layer in range(2):
+        edge = jnp.zeros((q * frames + 2, 1, padded, 3 * half), BF16)
+        taps[layer, :, 0:1] = edge
+        taps[layer, :, tall + 1 : tall + 2] = edge
+
+        @pl.when(t == n_t - 1)
+        def _(layer=layer):
+            def clear(f, carry):
+                taps[layer, q * frames + f] = jnp.zeros((tall + 2, padded, 3 * half), BF16)
+                return carry
+
+            lax.fori_loop(0, 2, clear, 0)
+
     grads[0, own_frames, own_rows] = cot_ref[:, :, :, mine]
 
     field_one = f_ref[...].reshape(rows, channels).astype(F32)
@@ -510,10 +509,10 @@
 
     take_fields(0)
     across(0).start()
+    across_land(0).wait_recv()
+    activate(0, 3)
     take_moves(moves_of[0], ("wide", "relay"))
     fill_rest(0)
-    across_land(0).wait_recv()
-    activate(0, 3)
     delta(0, d2)
     fill_own(1)
     conv(1, k1_ref, True)
@@ -546,8 +545,8 @@
         def _():
             block_copy(1, 1, 0).wait_recv()
             for k in range(1, nj):
-                for b in range(SOON, 3):
-                    pl.when(p + k >= nj)(lambda k=k, b=b: block_copy(1, k, b).start())
+                for b in range(1, 3):
+                    pl.when((p + k >= nj) & (b >= 2 - chan))(lambda k=k, b=b: block_copy(1, k, b).start())
 
     for layer, own, target in ((0, d2, d2_ref), (1, d1, d1_ref)):
         for b in range(3):

time: 49.3 us -> 49.3 us (level); the launches traced: 49.2 us -> 48.4 us
  Pallas kernels: 46.7 us -> 45.9 us
    pallas_call x1, Pallas kernels: 45.7 us -> 44.9 us  [shards(): pl.pallas_call(functools.partial(body, (width, n_t, n_s, q)), out_shape=s...]
where the time goes in v6:
time: 49.3 us; the launch traced here: 48.4 us
  Pallas kernels  45.9 us (93%)
  local copies, waits for them, and re-layouts  1.75 us (4%)
  between operations  0.72 us (1%)
    pallas_call x1, Pallas kernels, shards(): pl.pallas_call(functools.partial(body, (width, n_t, n_s, q)), out_shape=s...  44.9 us
    unnamed x9, local copies, waits for them, and re-layouts  1.65 us
    pallas_call x1, Pallas kernels, shards(): pl.pallas_call(hand_over, out_shape=shapes, in_specs=[vmem] * 4, out_spec...  1.01 us

profile of v6, /device:TPU:0, one launch (start us, length us, event | category | flops | bytes accessed | tf_op | source)
XLA Modules:
  0.0 48.4 jit_solution(7845370845556802136)
XLA Ops:
  0.6 0.0 copy-start.2
  0.6 0.0 copy-start.1
  0.7 1.1 %copy.10 = bf16[2,4,90,256]{3,2,1,0:T(8,128)(2,1)S(1)} copy(bf16[2,4,90,256]{3,1,2,0:T(4,128)(2,1)} %param.6) | data formatting | bytes 737280 | tf_op args[0]
  1.8 0.0 copy-start
  1.8 0.0 copy-done.1
  1.9 0.0 copy-done.2
  2.0 0.4 copy-done
  2.5 44.9 %shard_map.93 = (bf16[2,360,128]{2,1,0:T(8,128)(2,1)S(1)}, f32[3,3,3,32,128]{4,3,2,1,0:T(8,128)S(1)}, f32[3,3,3,32,128]{4,3,2,1,0:T(8,128)S(1)}, f32[2,128]{1,0:T(2,128)S(1)}) custom-call(bf16[2,4,96,256]{3,2,1,0:T(8,128)(2,1)S(1)} %pad.10.f_ref, bf16[2,4,96,256]{3,2,1,0:T(8,128)(2,1)S(1)} %pad.11.h_ref, bf16[2,4,96,256]{3,2,1,0:T(8,128)(2,1)S(1)} %pad.12.cot_ref, ...), custom_call_target="tpu_custom_call" | custom-call | tf_op jit(solution)/shard_map/pallas_call | solution.py:626
  47.4 1.0 %shard_map.94 = (bf16[2,360,128]{2,1,0:T(8,128)(2,1)}, f32[3,3,3,32,128]{4,3,2,1,0:T(8,128)}, f32[3,3,3,32,128]{4,3,2,1,0:T(8,128)}, f32[2,128]{1,0:T(2,128)}) custom-call(bf16[2,360,128]{2,1,0:T(8,128)(2,1)S(1)} %get-tuple-element.12.refs_0_, f32[3,3,3,32,128]{4,3,2,1,0:T(8,128)S(1)} %get-tuple-element.13.refs_1_, ...), custom_call_target="tpu_custom_call" | custom-call | tf_op jit(solution)/shard_map/pallas_call | solution.py:675
  (5 shorter events, 0.2 us)
Async XLA Ops:
  0.6 1.3 %copy-start.2 = (bf16[2,4,90,256]{3,1,2,0:T(4,128)(2,1)S(1)}, bf16[2,4,90,256]{3,1,2,0:T(4,128)(2,1)}, u32[]{:S(2)}) copy-start(bf16[2,4,90,256]{3,1,2,0:T(4,128)(2,1)} %param.8) | copy-start | bytes 1105924
  0.6 1.2 %copy-start.1 = (bf16[2,4,90,256]{3,1,2,0:T(4,128)(2,1)S(1)}, bf16[2,4,90,256]{3,1,2,0:T(4,128)(2,1)}, u32[]{:S(2)}) copy-start(bf16[2,4,90,256]{3,1,2,0:T(4,128)(2,1)} %param.7) | copy-start | bytes 1105924
  1.8 0.7 %copy-start = (f32[2,256]{1,0:T(2,128)S(1)}, f32[2,256]{1,0:T(2,128)}, u32[]{:S(2)}) copy-start(f32[2,256]{1,0:T(2,128)} %gain_hbm.1) | copy-start | bytes 6148
